TPU v7x, 128 devices: a whole 4x4x4 slice. The times are simulated.
128 devices in a mesh: row: 8 (over x_hi, z), col: 16 (over x_lo, y, core).
Axes of the slice: x: 4 (x_hi: 2, x_lo: 2; x = x_hi * 2 + x_lo), y: 4, z: 4, core: 2. Of those that a mesh axis runs over, the one named last changes fastest.
Arguments:
- tokens: bfloat16 [1024, 12288], P('row', 'col'), may hold values from -6 to 6
- prev_tokens: bfloat16 [1024, 12288], P('row', 'col'), may hold values from -6 to 6
- hidden_grad: bfloat16 [1024, 49152], P('col', 'row'), may hold values from -6 to 6
- active_blocks: int32 [1], replicated, may hold values from 6 to 16
- weight: bfloat16 [12288, 49152], P('col', 'row'), may hold values from -0.0546875 to 0.0546875
Outputs:
- activation: bfloat16 [1024, 49152], P('col', 'row')
- weight_grad: bfloat16 [12288, 49152], P('col', 'row')
Inputs may be any that keep to these rules, and one draw needn't show every extreme that they name: The sampled blocks are the first active_blocks[0] blocks of 3072 hidden units.
All inputs are finite; a program needn't handle non-finite values.
Results may differ from a plain program's by a relative error of at most 0.001.
Values may be sent and summed in bfloat16 or wider, within the bound.
No kernel may reach another device: no remote copies, remote signals or barrier semaphores. Data moves between devices by JAX's collectives and lax.ppermute only.
A program may use at most 640 MiB of HBM per device.

v0:
```python
import jax
import jax.numpy as jnp
from jax import lax
from jax.sharding import PartitionSpec as P

BLOCK = 3072


def in_one_piece(arrays, axis, dim, along):
    both = jnp.concatenate(arrays, axis=along)
    result, at, outs = (lax.all_gather(both, axis, axis=dim, tiled=True), 0, [])
    for a in arrays:
        outs.append(lax.slice_in_dim(result, at, at + a.shape[along], axis=along))
        at += a.shape[along]
    return tuple(outs)


def shards(tokens, prev_tokens, hidden_grad, active_blocks, weight):
    local_units = weight.shape[1]
    first_unit = lax.axis_index("row") * local_units
    unit_limit = active_blocks[0] * BLOCK
    unit_ids = first_unit + lax.iota(jnp.int32, local_units)
    unit_mask = (unit_ids < unit_limit).astype(jnp.float32)
    gathered, earlier = in_one_piece((tokens, prev_tokens), "row", 0, 1)
    hidden = lax.psum_scatter(
        jnp.dot(gathered, weight, preferred_element_type=jnp.float32),
        "col",
        scatter_dimension=0,
        tiled=True,
    )
    activation = (jax.nn.gelu(hidden, approximate=False) * unit_mask).astype(jnp.bfloat16)
    grad_sum = lax.dot_general(
        earlier,
        lax.all_gather(hidden_grad, "col", axis=0, tiled=True),
        (((0,), (0,)), ((), ())),
        preferred_element_type=jnp.float32,
    )
    weight_grad = (grad_sum * unit_mask).astype(jnp.bfloat16)
    return (activation, weight_grad)


def solution(mesh):
    return jax.shard_map(
        shards,
        mesh=mesh,
        in_specs=(P("row", "col"), P("row", "col"), P("col", "row"), P(), P("col", "row")),
        out_specs=(P("col", "row"), P("col", "row")),
        check_vma=False,
    )
```

profile of v0, /device:TPU:0, one launch (start us, length us, event | category | flops | bytes accessed | tf_op | source)
XLA Modules:
  0.0 303.0 jit_solution(265817429871638443)
XLA Ops:
  7.2 0.0 all-gather.3.cloned.1.call-start
  7.2 1.8 pad_maximum_fusion
  9.0 0.0 all-gather.3.cloned.1.call-update
  9.0 0.0 all-gather.5.cloned.1.call-start
  9.1 0.7 all-gather.5.cloned.1.call-update
  9.8 0.0 reduce-scatter.2.cloned.1.call-start
  9.8 66.0 %all-gather.3.cloned.1.call-done = bf16[1024,1536]{1,0:T(8,128)(2,1)} async-done(((bf16[128,1536]{1,0:T(8,128)(2,1)}), bf16[1024,1536]{1,0:T(8,128)(2,1)}) %all-gather.3.cloned.1.call-update) | async-done | bytes 3145744 | tf_op jit(solution)/shard_map/all_gather | solution.py:11
  75.8 17.5 %fusion.5 = f32[1024,6144]{1,0:T(8,128)} fusion(bf16[768,6144]{1,0:T(8,128)(2,1)} %param.9, bf16[1024,1536]{1,0:T(8,128)(2,1)} %all-gather.3.cloned.1.call-done), kind=kOutput, calls=%fused_computation.7 | convolution fusion | flops 9663676416 | bytes 36175872 | tf_op jit(solution)/shard_map/dot_general | solution.py:26
  93.3 0.0 copy-start
  93.3 0.0 reduce-scatter.2.cloned.1.call-update
  94.2 52.9 %all-gather.5.cloned.1.call-done = bf16[1024,6144]{1,0:T(8,128)(2,1)} async-done(((bf16[64,6144]{1,0:T(8,128)(2,1)}), bf16[1024,6144]{1,0:T(8,128)(2,1)}) %all-gather.5.cloned.1.call-update) | async-done | bytes 12582928 | tf_op jit(solution)/shard_map/all_gather | solution.py:34
  147.1 0.0 copy-done
  147.1 16.8 %multiply_convert_fusion = bf16[768,6144]{1,0:T(8,128)(2,1)} fusion(bf16[1024,6144]{1,0:T(8,128)(2,1)} %all-gather.5.cloned.1.call-done, f32[6144]{0:T(1024)S(1)} %fusion.14, bf16[1024,1536]{1,0:T(8,128)(2,1)S(1)} %copy-done), kind=kOutput, calls=%fused_computation | convolution fusion | flops 9673113600 | bytes 23617536 | tf_op jit(solution)/shard_map/dot_general | solution.py:32
  163.8 127.4 %reduce-scatter.2.cloned.1.call-done = f32[64,6144]{1,0:T(8,128)} async-done(((f32[1024,6144]{1,0:T(8,128)}), f32[64,6144]{1,0:T(8,128)}) %reduce-scatter.2.cloned.1.call-update) | async-done | bytes 1572880 | tf_op jit(solution)/shard_map/reduce_scatter | solution.py:25
  291.2 5.3 %fusion.3 = bf16[64,6144]{1,0:T(8,128)(2,1)} fusion(f32[64,6144]{1,0:T(8,128)} %reduce-scatter.2.cloned.1.call-done, f32[6144]{0:T(1024)S(1)} %fusion.14), kind=kLoop, calls=%fused_computation.5 | loop fusion | flops 25952256 | bytes 2383872 | tf_op jit(solution)/shard_map/convert_element_type | solution.py:31
  (1 shorter events, 0.0 us)
Async XLA Ops:
  7.2 68.6 %all-gather.3.cloned.1.call-start = ((), (), s32[]{:S(2)}) async-start(), calls=%async_computation.1 | async-start | bytes 3538944 | tf_op jit(solution)/shard_map/all_gather | solution.py:11
  9.0 138.0 %all-gather.5.cloned.1.call-start = ((), (), s32[]{:S(2)}) async-start(), calls=%async_computation.3 | async-start | bytes 13369344 | tf_op jit(solution)/shard_map/all_gather | solution.py:34
  9.8 281.4 %reduce-scatter.2.cloned.1.call-start = ((), (), s32[]{:S(2)}) async-start(), calls=%async_computation.2 | async-start | bytes 26738688 | tf_op jit(solution)/shard_map/reduce_scatter | solution.py:25
  93.3 53.7 %copy-start = (bf16[1024,1536]{1,0:T(8,128)(2,1)S(1)}, bf16[1024,1536]{1,0:T(8,128)(2,1)}, u32[]{:S(2)}) copy-start(bf16[1024,1536]{1,0:T(8,128)(2,1)} %all-gather.3.cloned.1.call-done) | copy-start | bytes 9437188
Sparse Core Ops, SparseCore 0:
  10.8 64.8 all-gather.2
  77.5 69.5 all-gather.4
  149.5 141.6 reduce-scatter.1
where the time goes:
time: 303 us
  waiting for transfers between devices  247 us (82%)
  matrix products  34.3 us (11%)
  between operations  14.6 us (5%)
  other arithmetic  7.08 us (2%)
    reduce_scatter x1, waiting for transfers between devices, shards(): lax.psum_scatter(jnp.dot(gathered, weight, preferred_element_type=jnp.flo...  127 us
    all_gather x1, waiting for transfers between devices, in_one_piece(): result, at, outs = (lax.all_gather(both, axis, axis=dim, tiled=True), 0, [])  66 us
    all_gather x1, waiting for transfers between devices, shards(): lax.all_gather(hidden_grad, 'col', axis=0, tiled=True)  52.9 us
    dot_general x1, matrix products, shards(): jnp.dot(gathered, weight, preferred_element_type=jnp.float32)  17.5 us
    dot_general x1, matrix products, shards(): lax.dot_general(earlier, lax.all_gather(hidden_grad, 'col', axis=0, tiled...  16.8 us
  transfers between devices with their start and end apart: 3, of which 3 were waited for; matrix products, arithmetic and copies ran while one was open for 11% of the time, Pallas kernels for 0%

commit v1 on v0

v1 whole, which is shorter than its diff:
```python
from functools import partial

import jax
import jax.numpy as jnp
from jax import lax
from jax.experimental import pallas as pl
from jax.experimental.pallas import tpu as pltpu
from jax.sharding import PartitionSpec as P


BLOCK = 3072
ROUND = 1.5 * 2.0 ** 23
F32, BF16, I16, I32 = jnp.float32, jnp.bfloat16, jnp.int16, jnp.int32


def perm(f):
    out = []
    for i in range(128):
        r, c = divmod(i, 16)
        xh, z, xl, y, k = f(r // 4, r % 4, c // 8, (c // 2) % 4, c % 2)
        out.append((i, (xh * 4 + z % 4) * 16 + xl * 8 + (y % 4) * 2 + k))
    return out


SIB = perm(lambda h, z, x, y, k: (h, z, x, y, 1 - k))
XLO = perm(lambda h, z, x, y, k: (h, z, 1 - x, y, k))
XHI = perm(lambda h, z, x, y, k: (1 - h, z, x, y, k))
YUP = perm(lambda h, z, x, y, k: (h, z, x, y + 1, k))
YDN = perm(lambda h, z, x, y, k: (h, z, x, y - 1, k))
YTWO = perm(lambda h, z, x, y, k: (h, z, x, y + 2, k))
ZUP = perm(lambda h, z, x, y, k: (h, z + 1, x, y, k))
ZDN = perm(lambda h, z, x, y, k: (h, z - 1, x, y, k))
ZTWO = perm(lambda h, z, x, y, k: (h, z + 2, x, y, k))


def send(a, p):
    return lax.ppermute(a, ("row", "col"), p)


OFFS = (0, -1, 1, 2)
TAG = 16
PART_LIMIT = 24
ROOT_HALF = 0.5 ** 0.5


def encode(v, ref, cols, base=0):
    rows = v.shape[0]
    top = jnp.maximum(jnp.max(jnp.abs(v), axis=0, keepdims=True), 2.0 ** -100)
    e = jnp.floor(jnp.log2(top * (1 + 2.0 ** -10))) + 1
    mant = jnp.ceil(top * jnp.exp2(15 - e))
    scale = mant * jnp.exp2(e - 15) * (1 / 32767)
    q = v * (1 / scale) + ROUND - ROUND
    ref[base:base + rows, cols] = q.astype(I32).astype(I16)
    sub = lax.broadcasted_iota(I32, (TAG, v.shape[1]), 0)
    ref[base + rows:base + rows + TAG, cols] = jnp.where(sub < TAG // 2, mant, e).astype(I32).astype(I16)


def decode(ref, rows, cols):
    n = ref.shape[0] - TAG
    tag = ref[n:, cols].astype(I32).astype(F32)
    scale = tag[0:1] * jnp.exp2(tag[TAG // 2:TAG // 2 + 1] - 15) * (1 / 32767)
    return ref[rows, cols].astype(I32).astype(F32) * scale


def over_columns(n, width, body):
    def step(i, c):
        body(pl.multiple_of(i * width, width))
        return c

    lax.fori_loop(0, n // width, step, 0)


def load_kernel(ids, w, w_far, own, sib, sems):
    half = own.shape[1]
    cols = pl.ds(pl.multiple_of(ids[0] * half, half), half)
    copies = [pltpu.make_async_copy(src.at[:, cols], dst, sems.at[i]) for i, (src, dst) in enumerate(((w, own), (w_far, sib)))]
    for c in copies:
        c.start()
    for c in copies:
        c.wait()


def part_kernel(ids, *refs):
    n = (len(refs) - 2) // 3
    own, sib, (w_own, w_sib), outs = refs[:n], refs[n:2 * n], refs[2 * n:2 * n + 2], refs[2 * n + 2:]
    slab, half = w_own.shape
    lhs = jnp.concatenate(
        [jnp.concatenate([a[...].reshape(256, slab), b[...].reshape(256, slab)], axis=1) for a, b in zip(own, sib)], axis=0
    )

    def block(c):
        cols = pl.ds(c, 512)
        part = jnp.dot(lhs, jnp.concatenate([w_own[:, cols], w_sib[:, cols]], axis=0), preferred_element_type=F32)
        for j, out in enumerate(outs):
            out[:, cols] = part[j * 256:(j + 1) * 256]

    for c in range(0, half, 512):
        block(c)


def with_part(ids, parts, off, f):
    k = lax.rem(ids[1] - ids[3] + off + 8, 4)
    for part, j in zip(parts, (0, 3, 1, 2)):
        pl.when(k == j)(lambda part=part: f(part))


def side(ids, s):
    return pl.ds(pl.multiple_of(lax.rem(ids[2] + ids[4] + 1 + s, 2) * 128, 128), 128)


def first_kernel(ids, *refs):
    parts, (m_up, m_dn) = refs[:4], refs[4:]
    h = m_up.shape[1]

    def f(part):
        def block(c):
            cols, far = pl.ds(c, 256), pl.ds(c + h, 256)
            for out, at in ((m_up, cols), (m_dn, far)):
                encode(jnp.concatenate([part[side(ids, 0), at], part[side(ids, 1), at]], axis=0), out, cols)

        over_columns(h, 256, block)

    with_part(ids, parts, 2, f)


def second_kernel(ids, *refs):
    parts, (up1, up2, dn1, dn2) = refs[:4], refs[4:]
    h = up1.shape[1]

    def go(part, one, two, base):
        def block(c):
            encode(part[side(ids, 0), pl.ds(c + base, 256)], one, pl.ds(c, 256))
            encode(part[side(ids, 1), pl.ds(c + base, 256)], two, pl.ds(c, 256))

        over_columns(h, 256, block)

    with_part(ids, parts, 1, lambda part: go(part, up1, up2, h))
    with_part(ids, parts, -1, lambda part: go(part, dn1, dn2, 0))


def relay_kernel(off, ids, *refs):
    parts, m, first, second = refs[:4], refs[4], refs[5], refs[6]
    h = m.shape[1]
    base = 0 if off == 1 else h

    def f(part):
        def block(c):
            cols, at = pl.ds(c, 256), pl.ds(c + base, 256)
            encode(part[side(ids, 0), at] + decode(m, slice(0, 128), cols), first, cols)
            encode(part[side(ids, 1), at] + decode(m, slice(128, 256), cols), second, cols)

        over_columns(h, 256, block)

    with_part(ids, parts, off, f)


def give_kernel(ids, *refs):
    parts, (m2_up, m2_dn, m3_up, m3_dn, out) = refs[:4], refs[4:]
    h = m2_up.shape[1]
    rows = slice(0, 128)

    def f(part):
        def block(c):
            cols, far = pl.ds(c, 256), pl.ds(c + h, 256)
            encode(part[side(ids, 0), cols] + (decode(m3_up, rows, cols) + decode(m2_dn, rows, cols)), out, cols)
            encode(part[side(ids, 0), far] + (decode(m2_up, rows, cols) + decode(m3_dn, rows, cols)), out, far)

        over_columns(h, 256, block)

    with_part(ids, parts, 0, f)


def keep_kernel(ids, *refs):
    parts, (m2_up, m2_dn, m3_up, m3_dn, x, own, sib) = refs[:4], refs[4:]
    h = m2_up.shape[1]
    core = ids[0]
    start = lax.rem(ids[2] + ids[4], 2) * 128

    def finish(v, at):
        unit = ids[5] + core * 2 * h + at + lax.broadcasted_iota(I32, (1, 256), 1)
        mask = (unit < ids[6]).astype(F32)
        return (0.5 * v * (1 + lax.erf(v * ROOT_HALF)) * mask).astype(BF16)

    def f(part):
        def block(c):
            cols, far = pl.ds(c, 256), pl.ds(c + h, 256)
            for out, mine in ((own, core), (sib, 1 - core)):
                rows = pl.ds(pl.multiple_of(mine * 64, 64), 64)
                base = pl.ds(pl.multiple_of(mine * 64 + start, 64), 64)
                v = part[base, cols] + (decode(m3_up, rows, cols) + decode(m2_dn, rows, cols)) + decode(x, rows, cols)
                out[:, cols] = finish(v, c)
                v = part[base, far] + (decode(m2_up, rows, cols) + decode(m3_dn, rows, cols)) + decode(x, rows, far)
                out[:, far] = finish(v, c + h)

        over_columns(h, 256, block)

    with_part(ids, parts, 0, f)


def earlier_kernel(ids, p0, p1, p2, p3, out, std):
    core, y, xl, z, xh = ids[0], ids[1], ids[2], ids[3], ids[4]
    for j, off in enumerate(OFFS):
        for s in range(2):
            at = lax.rem(z + off + 4, 4) * 2 + lax.rem(xh + s, 2)
            std[pl.ds(pl.multiple_of(at * 128, 128), 128), :] = (p0, p1, p2, p3)[j][s]
    for s in range(2):
        for j, off in enumerate(OFFS):
            at = lax.rem(y + off + 4, 4) * 2 + lax.rem(xl + s, 2)
            own = std[pl.ds(pl.multiple_of(at * 128 + core * 64, 64), 64), :]
            sib = std[pl.ds(pl.multiple_of(at * 128 + (1 - core) * 64, 64), 64), :]
            i = s * 4 + j
            out[:, i * 128:(i + 1) * 128] = jnp.concatenate([own, sib], axis=0).T


def grad_kernel(ids, *refs):
    own, sib, p_t, out, rhs = refs[:8], refs[8:16], refs[16], refs[17], refs[18]
    for j in range(8):
        rhs[j * 128:j * 128 + 64, :] = own[j][...]
        rhs[j * 128 + 64:j * 128 + 128, :] = sib[j][...]
    tn = out.shape[1]
    unit = ids[5] + pl.program_id(0) * tn + lax.broadcasted_iota(I32, (1, tn), 1)
    mask = (unit < ids[6]).astype(F32)
    grad = jnp.dot(p_t[...], rhs[...], preferred_element_type=F32)
    out[...] = (grad * mask).astype(BF16)


def vmem():
    return pl.BlockSpec(memory_space=pltpu.VMEM)


def shards(tokens, prev_tokens, hidden_grad, active_blocks, weight):
    slab, units = weight.shape
    half = units // 2
    row, col = lax.axis_index("row"), lax.axis_index("col")
    core = col % 2
    ids = jnp.stack([core, (col // 2) % 4, col // 8, row % 4, row // 4, row * units, active_blocks[0] * BLOCK, 0]).astype(I32)

    def call(f, outs, grid=(), specs=None, out_specs=None, scratch=(), flops=1 << 20, limit=16):
        params = pltpu.CompilerParams(vmem_limit_bytes=limit << 20)
        cost = pl.CostEstimate(flops=flops, bytes_accessed=1 << 20, transcendentals=0)
        spec = pltpu.PrefetchScalarGridSpec(num_scalar_prefetch=1, grid=grid, in_specs=specs, out_specs=out_specs, scratch_shapes=scratch)
        g = pl.pallas_call(f, grid_spec=spec, out_shape=outs, compiler_params=params, cost_estimate=cost)

        def run(*args):
            return g(ids, *args)

        return run

    def small(f, outs, *args):
        return call(f, outs, (), [vmem()] * len(args), [vmem()] * len(outs))(*args)

    def gather_row(a):
        near = jnp.stack([a, send(a, XHI)])
        return [near, send(near, ZUP), send(near, ZDN), send(near, ZTWO)]

    t_own = gather_row(tokens)
    t_sib = [send(a, SIB) for a in t_own]
    w_sib = send(weight, SIB)

    h_own = [hidden_grad, send(hidden_grad, YUP), send(hidden_grad, YDN), send(hidden_grad, YTWO)]
    h_own = h_own + [send(a, XLO) for a in h_own]
    h_sib = [send(a, SIB) for a in h_own]

    p_own = gather_row(prev_tokens)

    S = jax.ShapeDtypeStruct
    V = pltpu.VMEM
    quarter = half // 2
    hbm = pl.BlockSpec(memory_space=pltpu.HBM)
    w_half = V((slab, half), BF16)
    w_own, w_far = call(load_kernel, [w_half] * 2, (), [hbm] * 2, [vmem()] * 2, [pltpu.SemaphoreType.DMA((2,))])(weight, w_sib)

    def partials(which):
        n = len(which)
        args = [t_own[j] for j in which] + [t_sib[j] for j in which] + [w_own, w_far]
        return call(
            part_kernel, [V((256, half), F32)] * n, (), [vmem()] * len(args), [vmem()] * n,
            flops=2 * 256 * n * 2 * slab * half, limit=PART_LIMIT,
        )(*args)

    parts = partials((0,)) + partials((1, 2)) + partials((3,))
    msg, piece = V((256 + TAG, quarter), I16), V((128 + TAG, quarter), I16)
    m1_up, m1_dn = small(first_kernel, [msg] * 2, *parts)
    m1_up, m1_dn = send(m1_up, YUP), send(m1_dn, YDN)
    up1, up2, dn1, dn2 = small(second_kernel, [piece] * 4, *parts)
    m2_up1, m2_dn1 = send(up1, YUP), send(dn1, YDN)
    m2_up2, m2_dn2 = send(up2, YUP), send(dn2, YDN)
    m3_up1, m3_up2 = small(partial(relay_kernel, 1), [piece] * 2, *parts, m1_up)
    m3_dn1, m3_dn2 = small(partial(relay_kernel, -1), [piece] * 2, *parts, m1_dn)
    m3_up1, m3_dn1 = send(m3_up1, YUP), send(m3_dn1, YDN)
    m3_up2, m3_dn2 = send(m3_up2, YUP), send(m3_dn2, YDN)
    given, = small(give_kernel, [V((128 + TAG, half), I16)], *parts, m2_up1, m2_dn1, m3_up1, m3_dn1)
    x_in = send(given, XLO)
    act = V((64, half), BF16)
    act_own, act_give = small(keep_kernel, [act] * 2, *parts, m2_up2, m2_dn2, m3_up2, m3_dn2, x_in)
    act_sib = send(act_give, SIB)
    activation = jnp.where(core == 0, jnp.concatenate([act_own, act_sib], 1), jnp.concatenate([act_sib, act_own], 1))

    p_t, = call(earlier_kernel, [V((slab, 1024), BF16)], (), [vmem()] * 4, [vmem()], [V((1024, slab), BF16)])(*p_own)
    tg = 1024
    weight_grad = call(
        grad_kernel, S((slab, units), BF16), (units // tg,),
        [pl.BlockSpec((64, tg), lambda i, s: (0, i))] * 16 + [vmem()],
        pl.BlockSpec((slab, tg), lambda i, s: (0, i)), [V((1024, tg), BF16)],
        flops=2 * 1024 * slab * units, limit=24,
    )(*h_own, *h_sib, p_t)
    return (activation, weight_grad)


def solution(mesh):
    return jax.shard_map(
        shards,
        mesh=mesh,
        in_specs=(P("row", "col"), P("row", "col"), P("col", "row"), P(), P("col", "row")),
        out_specs=(P("col", "row"), P("col", "row")),
        check_vma=False,
    )
```

time: 303 us -> 232 us (0.77)
  waiting for transfers between devices: 247 us -> 107 us
  starting transfers between devices: 0.12 us -> 51 us
  Pallas kernels: 0 us -> 43.5 us
  matrix products: 34.3 us -> 0 us
  local copies, waits for them, and re-layouts: 0.01 us -> 25.5 us
  between operations: 14.6 us -> 1.73 us
  other arithmetic: 7.08 us -> 2.06 us
    reduce_scatter x1 -> x0, waiting for transfers between devices: 127 us -> none  [shards(): lax.psum_scatter(jnp.dot(gathered, weight, preferred_element_type=jnp.flo...]
    all_gather x2 -> x0, waiting for transfers between devices: 119 us -> none  [the longest x1 66 us: in_one_piece(): result, at, outs = (lax.all_gather(both, axis, axis=dim, tiled=True), 0, [])]
    ppermute x0 -> x40, waiting for transfers between devices: none -> 107 us  [send(): return lax.ppermute(a, ('row', 'col'), p)]
    ppermute x0 -> x40, starting transfers between devices: none -> 51 us  [send(): return lax.ppermute(a, ('row', 'col'), p)]
    pallas_call x0 -> x12, Pallas kernels: none -> 43.5 us  [run(): return g(ids, *args)]
    dot_general x2 -> x0, matrix products: 34.3 us -> none  [the longest x1 17.5 us: shards(): jnp.dot(gathered, weight, preferred_element_type=jnp.float32)]
    unnamed x2 -> x80, local copies, waits for them, and re-layouts: 0.01 us -> 25.4 us
    convert_element_type x2 -> x0, other arithmetic: 5.29 us -> none  [the longest x1 5.28 us: shards(): (jax.nn.gelu(hidden, approximate=False) * unit_mask).astype(jnp.bfloat16)]
  transfers between devices with their start and end apart: 3 -> 40, of which waited for: 3 -> 18; matrix products, arithmetic and copies ran while one was open for 11% -> 0% of each run, Pallas kernels for 0% -> 15%
where the time goes in v1:
time: 232 us; the launch traced here: 231 us
  waiting for transfers between devices  107 us (46%)
  starting transfers between devices  51 us (22%)
  Pallas kernels  43.5 us (19%)
  local copies, waits for them, and re-layouts  25.5 us (11%)
    ppermute x40, waiting for transfers between devices, send(): return lax.ppermute(a, ('row', 'col'), p)  107 us
    ppermute x40, starting transfers between devices, send(): return lax.ppermute(a, ('row', 'col'), p)  51 us
    pallas_call x12, Pallas kernels, run(): return g(ids, *args)  43.5 us
    unnamed x80, local copies, waits for them, and re-layouts  25.4 us
  transfers between devices with their start and end apart: 40, of which 18 were waited for; matrix products, arithmetic and copies ran while one was open for 0% of the time, Pallas kernels for 15%

profile of v1, /device:TPU:0, one launch (start us, length us, event | category | flops | bytes accessed | tf_op | source)
XLA Modules:
  0.0 230.6 jit_solution(2655323245557112268)
XLA Ops:
  0.7 3.2 %collective-permute-start = (bf16[128,768]{1,0:T(8,128)(2,1)}, bf16[128,768]{1,0:T(8,128)(2,1)S(1)}, u32[]{:S(2)}, u32[]{:S(2)}) collective-permute-start(bf16[128,768]{1,0:T(8,128)(2,1)} %param.5), channel_id=1, source_target_pairs={{0,64},{1,65},{2,66},{3,67},{4,68},{5,69},{6,70},{7,71},{8,72},{9,... | collective-permute-start | bytes 589832 | tf_op jit(solution)/shard_map/ppermute | solution.py:37
  3.9 5.8 %collective-permute-done = bf16[128,768]{1,0:T(8,128)(2,1)S(1)} collective-permute-done((bf16[128,768]{1,0:T(8,128)(2,1)}, bf16[128,768]{1,0:T(8,128)(2,1)S(1)}, u32[]{:S(2)}, u32[]{:S(2)}) %collective-permute-start) | collective-permute-done | bytes 196640 | tf_op jit(solution)/shard_map/ppermute | solution.py:37
  10.7 4.1 %collective-permute-start.7 = (bf16[2,128,768]{2,1,0:T(8,128)(2,1)S(1)}, bf16[2,128,768]{2,1,0:T(8,128)(2,1)S(1)}, u32[]{:S(2)}, u32[]{:S(2)}) collective-permute-start(bf16[2,128,768]{2,1,0:T(8,128)(2,1)S(1)} %pad_maximum_fusion.refs_0_), channel_id=1, source_target_pairs={{0,32},{1,33},{2,34},{3,35},{4,36},{5,37},{6,38},{7,39},{8,40},{9,... | collective-permute-start | bytes 1179656 | tf_op jit(solution)/shard_map/ppermute | solution.py:37
  18.0 6.8 %collective-permute-done.7.refs_0_ = bf16[2,128,768]{2,1,0:T(8,128)(2,1)S(1)} collective-permute-done((bf16[2,128,768]{2,1,0:T(8,128)(2,1)S(1)}, bf16[2,128,768]{2,1,0:T(8,128)(2,1)S(1)}, u32[]{:S(2)}, u32[]{:S(2)}) %collective-permute-start.7) | collective-permute-done | bytes 393248 | tf_op jit(solution)/shard_map/ppermute | solution.py:37
  26.1 6.1 %collective-permute-done.3.refs_0_ = bf16[2,128,768]{2,1,0:T(8,128)(2,1)} collective-permute-done((bf16[2,128,768]{2,1,0:T(8,128)(2,1)S(1)}, bf16[2,128,768]{2,1,0:T(8,128)(2,1)}, u32[]{:S(2)}, u32[]{:S(2)}) %collective-permute-start.3) | collective-permute-done | bytes 393248 | tf_op jit(solution)/shard_map/ppermute | solution.py:37
  32.9 3.7 %copy-done.6 = bf16[768,6144]{1,0:T(8,128)(2,1)S(1)} copy-done((bf16[768,6144]{1,0:T(8,128)(2,1)S(1)}, bf16[768,6144]{1,0:T(8,128)(2,1)}, u32[]{:S(2)}) %copy-start.6) | copy-done | bytes 9437208
  36.6 3.8 %shard_map.68 = (bf16[768,3072]{1,0:T(8,128)(2,1)S(1)}, bf16[768,3072]{1,0:T(8,128)(2,1)S(1)}) custom-call(s32[8]{0:T(128)S(1)} %stack.46.ids, bf16[768,6144]{1,0:T(8,128)(2,1)S(1)} %copy-done.6, bf16[768,6144]{1,0:T(8,128)(2,1)} %collective-permute-done.2.w_far), custom_call_target="tpu_custom_call" | custom-call | flops 1048576 | bytes 1048576 | tf_op jit(solution)/shard_map/pallas_call | solution.py:245
  46.3 4.2 %shard_map.69.refs_0_ = f32[256,3072]{1,0:T(8,128)S(1)} custom-call(s32[8]{0:T(128)S(1)} %stack.46.ids, bf16[2,128,768]{2,1,0:T(8,128)(2,1)S(1)} %pad_maximum_fusion.refs_0_, bf16[2,128,768]{2,1,0:T(8,128)(2,1)} %collective-permute-done.1.refs_1_, bf16[768,3072]{1,0:T(8,128)(2,1)S(1)} %get-tuple-element.18.refs_2_.refs_4_, ...), custom_call_target="tpu_custom_call" | custom-call | flops 2415919104 | bytes 1048576 | tf_op jit(solution)/shard_map/pallas_call | solution.py:245
  50.6 7.2 %shard_map.70 = (f32[256,3072]{1,0:T(8,128)S(1)}, f32[256,3072]{1,0:T(8,128)S(1)}) custom-call(s32[8]{0:T(128)S(1)} %stack.46.ids, bf16[2,128,768]{2,1,0:T(8,128)(2,1)} %collective-permute-done.3.refs_0_, bf16[2,128,768]{2,1,0:T(8,128)(2,1)} %collective-permute-done.4.refs_1_, bf16[2,128,768]{2,1,0:T(8,128)(2,1)S(1)} %collective-permute-done.5.refs_2_, ...), custom_call_target="tpu_custom_call" | custom-call | flops 4831838208 | bytes 1048576 | tf_op jit(solution)/shard_map/pallas_call | solution.py:245
  65.6 5.5 %collective-permute-done.36 = bf16[128,768]{1,0:T(8,128)(2,1)S(1)} collective-permute-done((bf16[128,768]{1,0:T(8,128)(2,1)S(1)}, bf16[128,768]{1,0:T(8,128)(2,1)S(1)}, u32[]{:S(2)}, u32[]{:S(2)}) %collective-permute-start.36) | collective-permute-done | bytes 196640 | tf_op jit(solution)/shard_map/ppermute | solution.py:37
  75.3 8.2 %collective-permute-done.37.p1 = bf16[2,128,768]{2,1,0:T(8,128)(2,1)S(1)} collective-permute-done((bf16[2,128,768]{2,1,0:T(8,128)(2,1)S(1)}, bf16[2,128,768]{2,1,0:T(8,128)(2,1)S(1)}, u32[]{:S(2)}, u32[]{:S(2)}) %collective-permute-start.37) | collective-permute-done | bytes 393248 | tf_op jit(solution)/shard_map/ppermute | solution.py:37
  83.9 6.7 %collective-permute-done.38.p2 = bf16[2,128,768]{2,1,0:T(8,128)(2,1)S(1)} collective-permute-done((bf16[2,128,768]{2,1,0:T(8,128)(2,1)S(1)}, bf16[2,128,768]{2,1,0:T(8,128)(2,1)S(1)}, u32[]{:S(2)}, u32[]{:S(2)}) %collective-permute-start.38) | collective-permute-done | bytes 393248 | tf_op jit(solution)/shard_map/ppermute | solution.py:37
  99.8 6.2 %collective-permute-done.21.refs_1_ = bf16[64,6144]{1,0:T(8,128)(2,1)S(1)} collective-permute-done((bf16[64,6144]{1,0:T(8,128)(2,1)S(1)}, bf16[64,6144]{1,0:T(8,128)(2,1)S(1)}, u32[]{:S(2)}, u32[]{:S(2)}) %collective-permute-start.21) | collective-permute-done | bytes 786464 | tf_op jit(solution)/shard_map/ppermute | solution.py:37
  106.1 12.9 %collective-permute-done.22.refs_2_ = bf16[64,6144]{1,0:T(8,128)(2,1)S(1)} collective-permute-done((bf16[64,6144]{1,0:T(8,128)(2,1)S(1)}, bf16[64,6144]{1,0:T(8,128)(2,1)S(1)}, u32[]{:S(2)}, u32[]{:S(2)}) %collective-permute-start.22) | collective-permute-done | bytes 786464 | tf_op jit(solution)/shard_map/ppermute | solution.py:37
  119.0 4.2 %collective-permute-start.16 = (s16[144,1536]{1,0:T(8,128)(2,1)S(1)}, s16[144,1536]{1,0:T(8,128)(2,1)S(1)}, u32[]{:S(2)}, u32[]{:S(2)}) collective-permute-start(s16[144,1536]{1,0:T(8,128)(2,1)S(1)} %get-tuple-element.29), channel_id=1, source_target_pairs={{0,6},{1,7},{2,0},{3,1},{4,2},{5,3},{6,4},{7,5},{8,14},{9,15},{10,... | collective-permute-start | bytes 1327112 | tf_op jit(solution)/shard_map/ppermute | solution.py:37
  123.4 6.9 %collective-permute-start.18 = (s16[144,1536]{1,0:T(8,128)(2,1)S(1)}, s16[144,1536]{1,0:T(8,128)(2,1)S(1)}, u32[]{:S(2)}, u32[]{:S(2)}) collective-permute-start(s16[144,1536]{1,0:T(8,128)(2,1)S(1)} %get-tuple-element.31), channel_id=1, source_target_pairs={{0,6},{1,7},{2,0},{3,1},{4,2},{5,3},{6,4},{7,5},{8,14},{9,15},{10,... | collective-permute-start | bytes 1327112 | tf_op jit(solution)/shard_map/ppermute | solution.py:37
  135.1 3.2 %collective-permute-done.18.refs_7_ = s16[144,1536]{1,0:T(8,128)(2,1)S(1)} collective-permute-done((s16[144,1536]{1,0:T(8,128)(2,1)S(1)}, s16[144,1536]{1,0:T(8,128)(2,1)S(1)}, u32[]{:S(2)}, u32[]{:S(2)}) %collective-permute-start.18) | collective-permute-done | bytes 442400 | tf_op jit(solution)/shard_map/ppermute | solution.py:37
  141.5 9.4 %collective-permute-done.25.refs_5_ = bf16[64,6144]{1,0:T(8,128)(2,1)} collective-permute-done((bf16[64,6144]{1,0:T(8,128)(2,1)S(1)}, bf16[64,6144]{1,0:T(8,128)(2,1)}, u32[]{:S(2)}, u32[]{:S(2)}) %collective-permute-start.25) | collective-permute-done | bytes 786464 | tf_op jit(solution)/shard_map/ppermute | solution.py:37
  152.4 15.3 %collective-permute-done.26.refs_6_ = bf16[64,6144]{1,0:T(8,128)(2,1)} collective-permute-done((bf16[64,6144]{1,0:T(8,128)(2,1)S(1)}, bf16[64,6144]{1,0:T(8,128)(2,1)}, u32[]{:S(2)}, u32[]{:S(2)}) %collective-permute-start.26) | collective-permute-done | bytes 786464 | tf_op jit(solution)/shard_map/ppermute | solution.py:37
  167.8 3.1 %collective-permute-start.10 = (s16[144,1536]{1,0:T(8,128)(2,1)S(1)}, s16[144,1536]{1,0:T(8,128)(2,1)S(1)}, u32[]{:S(2)}, u32[]{:S(2)}) collective-permute-start(s16[144,1536]{1,0:T(8,128)(2,1)S(1)} %get-tuple-element.23), channel_id=1, source_target_pairs={{0,6},{1,7},{2,0},{3,1},{4,2},{5,3},{6,4},{7,5},{8,14},{9,15},{10,... | collective-permute-start | bytes 1327112 | tf_op jit(solution)/shard_map/ppermute | solution.py:37
  170.9 11.1 %collective-permute-done.27.refs_7_ = bf16[64,6144]{1,0:T(8,128)(2,1)} collective-permute-done((bf16[64,6144]{1,0:T(8,128)(2,1)}, bf16[64,6144]{1,0:T(8,128)(2,1)}, u32[]{:S(2)}, u32[]{:S(2)}) %collective-permute-start.27) | collective-permute-done | bytes 786464 | tf_op jit(solution)/shard_map/ppermute | solution.py:37
  182.9 3.2 %collective-permute-start.14 = (s16[144,1536]{1,0:T(8,128)(2,1)S(1)}, s16[144,1536]{1,0:T(8,128)(2,1)S(1)}, u32[]{:S(2)}, u32[]{:S(2)}) collective-permute-start(s16[144,1536]{1,0:T(8,128)(2,1)S(1)} %get-tuple-element.27), channel_id=1, source_target_pairs={{0,6},{1,7},{2,0},{3,1},{4,2},{5,3},{6,4},{7,5},{8,14},{9,15},{10,... | collective-permute-start | bytes 1327112 | tf_op jit(solution)/shard_map/ppermute | solution.py:37
  187.9 3.6 %collective-permute-done.9.refs_4_ = s16[144,1536]{1,0:T(8,128)(2,1)S(1)} collective-permute-done((s16[144,1536]{1,0:T(8,128)(2,1)S(1)}, s16[144,1536]{1,0:T(8,128)(2,1)S(1)}, u32[]{:S(2)}, u32[]{:S(2)}) %collective-permute-start.9) | collective-permute-done | bytes 442400 | tf_op jit(solution)/shard_map/ppermute | solution.py:37
  215.0 14.5 %shard_map.79 = bf16[768,6144]{1,0:T(8,128)(2,1)} custom-call(s32[8]{0:T(128)S(1)} %stack.46.ids, bf16[64,6144]{1,0:T(8,128)(2,1)S(1)} %copy-done.28, bf16[64,6144]{1,0:T(8,128)(2,1)S(1)} %copy-done.30, bf16[64,6144]{1,0:T(8,128)(2,1)S(1)} %copy-done.32, bf16[64,6144]{1,0:T(8,128)(2,1)} %collective-permute-done.23.refs_3_, ...), custom_call_target="tpu_custom_call" | custom-call | flops 9663676416 | bytes 1048576 | tf_op jit(solution)/shard_map/pallas_call | solution.py:245
  (152 shorter events, 69.8 us)
Async XLA Ops:
  0.6 32.3 %collective-permute-start.2 = (bf16[768,6144]{1,0:T(8,128)(2,1)}, bf16[768,6144]{1,0:T(8,128)(2,1)}, u32[]{:S(2)}, u32[]{:S(2)}) collective-permute-start(bf16[768,6144]{1,0:T(8,128)(2,1)} %w.1), channel_id=1, source_target_pairs={{0,1},{1,0},{2,3},{3,2},{4,5},{5,4},{6,7},{7,6},{8,9},{9,8},{10,11... | collective-permute-start | bytes 28311560 | tf_op jit(solution)/shard_map/ppermute | solution.py:37
  24.8 21.5 %collective-permute-start.1 = (bf16[2,128,768]{2,1,0:T(8,128)(2,1)S(1)}, bf16[2,128,768]{2,1,0:T(8,128)(2,1)}, u32[]{:S(2)}, u32[]{:S(2)}) collective-permute-start(bf16[2,128,768]{2,1,0:T(8,128)(2,1)S(1)} %pad_maximum_fusion.refs_0_), channel_id=1, source_target_pairs={{0,1},{1,0},{2,3},{3,2},{4,5},{5,4},{6,7},{7,6},{8,9},{9,8},{10,11... | collective-permute-start | bytes 1179656 | tf_op jit(solution)/shard_map/ppermute | solution.py:37
  32.1 18.4 %collective-permute-start.5 = (bf16[2,128,768]{2,1,0:T(8,128)(2,1)}, bf16[2,128,768]{2,1,0:T(8,128)(2,1)S(1)}, u32[]{:S(2)}, u32[]{:S(2)}) collective-permute-start(bf16[2,128,768]{2,1,0:T(8,128)(2,1)} %collective-permute-done.3.refs_0_), channel_id=1, source_target_pairs={{0,1},{1,0},{2,3},{3,2},{4,5},{5,4},{6,7},{7,6},{8,9},{9,8},{10,11... | collective-permute-start | bytes 1179656 | tf_op jit(solution)/shard_map/ppermute | solution.py:37
  32.9 17.6 %collective-permute-start.6 = (bf16[2,128,768]{2,1,0:T(8,128)(2,1)}, bf16[2,128,768]{2,1,0:T(8,128)(2,1)S(1)}, u32[]{:S(2)}, u32[]{:S(2)}) collective-permute-start(bf16[2,128,768]{2,1,0:T(8,128)(2,1)} %collective-permute-done.4.refs_1_), channel_id=1, source_target_pairs={{0,1},{1,0},{2,3},{3,2},{4,5},{5,4},{6,7},{7,6},{8,9},{9,8},{10,11... | collective-permute-start | bytes 1179656 | tf_op jit(solution)/shard_map/ppermute | solution.py:37
  59.5 34.2 %collective-permute-start.13 = (s16[272,1536]{1,0:T(8,128)(2,1)S(1)}, s16[272,1536]{1,0:T(8,128)(2,1)S(1)}, u32[]{:S(2)}, u32[]{:S(2)}) collective-permute-start(s16[272,1536]{1,0:T(8,128)(2,1)S(1)} %get-tuple-element.26), channel_id=1, source_target_pairs={{0,6},{1,7},{2,0},{3,1},{4,2},{5,3},{6,4},{7,5},{8,14},{9,15},{10,... | collective-permute-start | bytes 2506760 | tf_op jit(solution)/shard_map/ppermute | solution.py:37
  62.6 32.7 %collective-permute-start.11 = (s16[272,1536]{1,0:T(8,128)(2,1)S(1)}, s16[272,1536]{1,0:T(8,128)(2,1)S(1)}, u32[]{:S(2)}, u32[]{:S(2)}) collective-permute-start(s16[272,1536]{1,0:T(8,128)(2,1)S(1)} %get-tuple-element.24), channel_id=1, source_target_pairs={{0,2},{1,3},{2,4},{3,5},{4,6},{5,7},{6,0},{7,1},{8,10},{9,11},{10,... | collective-permute-start | bytes 2506760 | tf_op jit(solution)/shard_map/ppermute | solution.py:37
  72.3 18.3 %collective-permute-start.38 = (bf16[2,128,768]{2,1,0:T(8,128)(2,1)S(1)}, bf16[2,128,768]{2,1,0:T(8,128)(2,1)S(1)}, u32[]{:S(2)}, u32[]{:S(2)}) collective-permute-start(bf16[2,128,768]{2,1,0:T(8,128)(2,1)S(1)} %pad_maximum_fusion.1.p0), channel_id=1, source_target_pairs={{0,48},{1,49},{2,50},{3,51},{4,52},{5,53},{6,54},{7,55},{8,56},{9,... | collective-permute-start | bytes 1179656 | tf_op jit(solution)/shard_map/ppermute | solution.py:37
  74.5 18.7 %collective-permute-start.39 = (bf16[2,128,768]{2,1,0:T(8,128)(2,1)S(1)}, bf16[2,128,768]{2,1,0:T(8,128)(2,1)S(1)}, u32[]{:S(2)}, u32[]{:S(2)}) collective-permute-start(bf16[2,128,768]{2,1,0:T(8,128)(2,1)S(1)} %pad_maximum_fusion.1.p0), channel_id=1, source_target_pairs={{0,32},{1,33},{2,34},{3,35},{4,36},{5,37},{6,38},{7,39},{8,40},{9,... | collective-permute-start | bytes 1179656 | tf_op jit(solution)/shard_map/ppermute | solution.py:37
  83.6 22.5 %collective-permute-start.21 = (bf16[64,6144]{1,0:T(8,128)(2,1)S(1)}, bf16[64,6144]{1,0:T(8,128)(2,1)S(1)}, u32[]{:S(2)}, u32[]{:S(2)}) collective-permute-start(bf16[64,6144]{1,0:T(8,128)(2,1)S(1)} %copy-done.27), channel_id=1, source_target_pairs={{0,2},{1,3},{2,4},{3,5},{4,6},{5,7},{6,0},{7,1},{8,10},{9,11},{10,... | collective-permute-start | bytes 2359304 | tf_op jit(solution)/shard_map/ppermute | solution.py:37
  90.5 28.4 %collective-permute-start.22 = (bf16[64,6144]{1,0:T(8,128)(2,1)S(1)}, bf16[64,6144]{1,0:T(8,128)(2,1)S(1)}, u32[]{:S(2)}, u32[]{:S(2)}) collective-permute-start(bf16[64,6144]{1,0:T(8,128)(2,1)S(1)} %copy-done.27), channel_id=1, source_target_pairs={{0,6},{1,7},{2,0},{3,1},{4,2},{5,3},{6,4},{7,5},{8,14},{9,15},{10,... | collective-permute-start | bytes 2359304 | tf_op jit(solution)/shard_map/ppermute | solution.py:37
  93.2 30.2 %collective-permute-start.23 = (bf16[64,6144]{1,0:T(8,128)(2,1)S(1)}, bf16[64,6144]{1,0:T(8,128)(2,1)}, u32[]{:S(2)}, u32[]{:S(2)}) collective-permute-start(bf16[64,6144]{1,0:T(8,128)(2,1)S(1)} %copy-done.27), channel_id=1, source_target_pairs={{0,4},{1,5},{2,6},{3,7},{4,0},{5,1},{6,2},{7,3},{8,12},{9,13},{10,... | collective-permute-start | bytes 2359304 | tf_op jit(solution)/shard_map/ppermute | solution.py:37
  93.8 36.5 %collective-permute-start.24 = (bf16[64,6144]{1,0:T(8,128)(2,1)S(1)}, bf16[64,6144]{1,0:T(8,128)(2,1)}, u32[]{:S(2)}, u32[]{:S(2)}) collective-permute-start(bf16[64,6144]{1,0:T(8,128)(2,1)S(1)} %copy-done.27), channel_id=1, source_target_pairs={{0,8},{1,9},{2,10},{3,11},{4,12},{5,13},{6,14},{7,15},{8,0},{9,1},... | collective-permute-start | bytes 2359304 | tf_op jit(solution)/shard_map/ppermute | solution.py:37
  95.3 35.0 %collective-permute-start.28 = (bf16[64,6144]{1,0:T(8,128)(2,1)S(1)}, bf16[64,6144]{1,0:T(8,128)(2,1)S(1)}, u32[]{:S(2)}, u32[]{:S(2)}) collective-permute-start(bf16[64,6144]{1,0:T(8,128)(2,1)S(1)} %copy-done.27), channel_id=1, source_target_pairs={{0,1},{1,0},{2,3},{3,2},{4,5},{5,4},{6,7},{7,6},{8,9},{9,8},{10,11... | collective-permute-start | bytes 2359304 | tf_op jit(solution)/shard_map/ppermute | solution.py:37
  106.0 25.9 %collective-permute-start.15 = (s16[144,1536]{1,0:T(8,128)(2,1)S(1)}, s16[144,1536]{1,0:T(8,128)(2,1)S(1)}, u32[]{:S(2)}, u32[]{:S(2)}) collective-permute-start(s16[144,1536]{1,0:T(8,128)(2,1)S(1)} %get-tuple-element.28), channel_id=1, source_target_pairs={{0,2},{1,3},{2,4},{3,5},{4,6},{5,7},{6,0},{7,1},{8,10},{9,11},{10,... | collective-permute-start | bytes 1327112 | tf_op jit(solution)/shard_map/ppermute | solution.py:37
  130.3 20.6 %collective-permute-start.25 = (bf16[64,6144]{1,0:T(8,128)(2,1)S(1)}, bf16[64,6144]{1,0:T(8,128)(2,1)}, u32[]{:S(2)}, u32[]{:S(2)}) collective-permute-start(bf16[64,6144]{1,0:T(8,128)(2,1)S(1)} %collective-permute-done.21.refs_1_), channel_id=1, source_target_pairs={{0,8},{1,9},{2,10},{3,11},{4,12},{5,13},{6,14},{7,15},{8,0},{9,1},... | collective-permute-start | bytes 2359304 | tf_op jit(solution)/shard_map/ppermute | solution.py:37
  131.9 35.8 %collective-permute-start.26 = (bf16[64,6144]{1,0:T(8,128)(2,1)S(1)}, bf16[64,6144]{1,0:T(8,128)(2,1)}, u32[]{:S(2)}, u32[]{:S(2)}) collective-permute-start(bf16[64,6144]{1,0:T(8,128)(2,1)S(1)} %collective-permute-done.22.refs_2_), channel_id=1, source_target_pairs={{0,8},{1,9},{2,10},{3,11},{4,12},{5,13},{6,14},{7,15},{8,0},{9,1},... | collective-permute-start | bytes 2359304 | tf_op jit(solution)/shard_map/ppermute | solution.py:37
  133.6 48.4 %collective-permute-start.27 = (bf16[64,6144]{1,0:T(8,128)(2,1)}, bf16[64,6144]{1,0:T(8,128)(2,1)}, u32[]{:S(2)}, u32[]{:S(2)}) collective-permute-start(bf16[64,6144]{1,0:T(8,128)(2,1)} %collective-permute-done.23.refs_3_), channel_id=1, source_target_pairs={{0,8},{1,9},{2,10},{3,11},{4,12},{5,13},{6,14},{7,15},{8,0},{9,1},... | collective-permute-start | bytes 2359304 | tf_op jit(solution)/shard_map/ppermute | solution.py:37
  138.4 43.7 %collective-permute-start.29 = (bf16[64,6144]{1,0:T(8,128)(2,1)S(1)}, bf16[64,6144]{1,0:T(8,128)(2,1)S(1)}, u32[]{:S(2)}, u32[]{:S(2)}) collective-permute-start(bf16[64,6144]{1,0:T(8,128)(2,1)S(1)} %collective-permute-done.21.refs_1_), channel_id=1, source_target_pairs={{0,1},{1,0},{2,3},{3,2},{4,5},{5,4},{6,7},{7,6},{8,9},{9,8},{10,11... | collective-permute-start | bytes 2359304 | tf_op jit(solution)/shard_map/ppermute | solution.py:37
  139.8 46.4 %collective-permute-start.30 = (bf16[64,6144]{1,0:T(8,128)(2,1)S(1)}, bf16[64,6144]{1,0:T(8,128)(2,1)S(1)}, u32[]{:S(2)}, u32[]{:S(2)}) collective-permute-start(bf16[64,6144]{1,0:T(8,128)(2,1)S(1)} %collective-permute-done.22.refs_2_), channel_id=1, source_target_pairs={{0,1},{1,0},{2,3},{3,2},{4,5},{5,4},{6,7},{7,6},{8,9},{9,8},{10,11... | collective-permute-start | bytes 2359304 | tf_op jit(solution)/shard_map/ppermute | solution.py:37
  150.9 46.5 %collective-permute-start.19 = (s16[144,3072]{1,0:T(8,128)(2,1)S(1)}, s16[144,3072]{1,0:T(8,128)(2,1)S(1)}, u32[]{:S(2)}, u32[]{:S(2)}) collective-permute-start(s16[144,3072]{1,0:T(8,128)(2,1)S(1)} %shard_map.76), channel_id=1, source_target_pairs={{0,8},{1,9},{2,10},{3,11},{4,12},{5,13},{6,14},{7,15},{8,0},{9,1},... | collective-permute-start | bytes 2654216 | tf_op jit(solution)/shard_map/ppermute | solution.py:37
  167.8 19.3 %collective-permute-start.10 = (s16[144,1536]{1,0:T(8,128)(2,1)S(1)}, s16[144,1536]{1,0:T(8,128)(2,1)S(1)}, u32[]{:S(2)}, u32[]{:S(2)}) collective-permute-start(s16[144,1536]{1,0:T(8,128)(2,1)S(1)} %get-tuple-element.23), channel_id=1, source_target_pairs={{0,6},{1,7},{2,0},{3,1},{4,2},{5,3},{6,4},{7,5},{8,14},{9,15},{10,... | collective-permute-start | bytes 1327112 | tf_op jit(solution)/shard_map/ppermute | solution.py:37
  187.9 26.6 %collective-permute-start.31 = (bf16[64,6144]{1,0:T(8,128)(2,1)}, bf16[64,6144]{1,0:T(8,128)(2,1)}, u32[]{:S(2)}, u32[]{:S(2)}) collective-permute-start(bf16[64,6144]{1,0:T(8,128)(2,1)} %collective-permute-done.23.refs_3_), channel_id=1, source_target_pairs={{0,1},{1,0},{2,3},{3,2},{4,5},{5,4},{6,7},{7,6},{8,9},{9,8},{10,11... | collective-permute-start | bytes 2359304 | tf_op jit(solution)/shard_map/ppermute | solution.py:37
  192.3 22.3 %collective-permute-start.32 = (bf16[64,6144]{1,0:T(8,128)(2,1)}, bf16[64,6144]{1,0:T(8,128)(2,1)}, u32[]{:S(2)}, u32[]{:S(2)}) collective-permute-start(bf16[64,6144]{1,0:T(8,128)(2,1)} %collective-permute-done.24.refs_4_), channel_id=1, source_target_pairs={{0,1},{1,0},{2,3},{3,2},{4,5},{5,4},{6,7},{7,6},{8,9},{9,8},{10,11... | collective-permute-start | bytes 2359304 | tf_op jit(solution)/shard_map/ppermute | solution.py:37
  193.1 21.5 %collective-permute-start.33 = (bf16[64,6144]{1,0:T(8,128)(2,1)}, bf16[64,6144]{1,0:T(8,128)(2,1)}, u32[]{:S(2)}, u32[]{:S(2)}) collective-permute-start(bf16[64,6144]{1,0:T(8,128)(2,1)} %collective-permute-done.25.refs_5_), channel_id=1, source_target_pairs={{0,1},{1,0},{2,3},{3,2},{4,5},{5,4},{6,7},{7,6},{8,9},{9,8},{10,11... | collective-permute-start | bytes 2359304 | tf_op jit(solution)/shard_map/ppermute | solution.py:37
  (56 other events, 641.0 us)

commit v2 on v1

--- a/solution.py
+++ b/solution.py
@@ -24,6 +24,7 @@
 
 SIB = perm(lambda h, z, x, y, k: (h, z, x, y, 1 - k))
 XLO = perm(lambda h, z, x, y, k: (h, z, 1 - x, y, k))
+XLO_SIB = perm(lambda h, z, x, y, k: (h, z, 1 - x, y, 1 - k))
 XHI = perm(lambda h, z, x, y, k: (1 - h, z, x, y, k))
 YUP = perm(lambda h, z, x, y, k: (h, z, x, y + 1, k))
 YDN = perm(lambda h, z, x, y, k: (h, z, x, y - 1, k))
@@ -38,8 +39,8 @@
 
 
 OFFS = (0, -1, 1, 2)
-TAG = 16
-PART_LIMIT = 24
+TAG = 8
+PART_LIMIT = 12
 ROOT_HALF = 0.5 ** 0.5
 
 
@@ -70,14 +71,11 @@
     lax.fori_loop(0, n // width, step, 0)
 
 
-def load_kernel(ids, w, w_far, own, sib, sems):
-    half = own.shape[1]
-    cols = pl.ds(pl.multiple_of(ids[0] * half, half), half)
-    copies = [pltpu.make_async_copy(src.at[:, cols], dst, sems.at[i]) for i, (src, dst) in enumerate(((w, own), (w_far, sib)))]
-    for c in copies:
-        c.start()
-    for c in copies:
-        c.wait()
+def load_kernel(ids, w, out, sem):
+    half = out.shape[1]
+    copy = pltpu.make_async_copy(w.at[:, pl.ds(pl.multiple_of(ids[0] * half, half), half)], out, sem.at[0])
+    copy.start()
+    copy.wait()
 
 
 def part_kernel(ids, *refs):
@@ -124,30 +122,30 @@
 
 
 def second_kernel(ids, *refs):
-    parts, (up1, up2, dn1, dn2) = refs[:4], refs[4:]
-    h = up1.shape[1]
-
-    def go(part, one, two, base):
-        def block(c):
-            encode(part[side(ids, 0), pl.ds(c + base, 256)], one, pl.ds(c, 256))
-            encode(part[side(ids, 1), pl.ds(c + base, 256)], two, pl.ds(c, 256))
+    parts, (up, dn) = refs[:4], refs[4:]
+    h = up.shape[1]
+
+    def go(part, out, base):
+        def block(c):
+            encode(part[side(ids, 0), pl.ds(c + base, 256)], out, pl.ds(c, 256))
 
         over_columns(h, 256, block)
 
-    with_part(ids, parts, 1, lambda part: go(part, up1, up2, h))
-    with_part(ids, parts, -1, lambda part: go(part, dn1, dn2, 0))
+    with_part(ids, parts, 1, lambda part: go(part, up, h))
+    with_part(ids, parts, -1, lambda part: go(part, dn, 0))
 
 
 def relay_kernel(off, ids, *refs):
     parts, m, first, second = refs[:4], refs[4], refs[5], refs[6]
     h = m.shape[1]
-    base = 0 if off == 1 else h
+    base, rest = (0, h) if off == 1 else (h, 0)
 
     def f(part):
         def block(c):
-            cols, at = pl.ds(c, 256), pl.ds(c + base, 256)
+            cols, at, other = pl.ds(c, 256), pl.ds(c + base, 256), pl.ds(c + rest, 256)
             encode(part[side(ids, 0), at] + decode(m, slice(0, 128), cols), first, cols)
-            encode(part[side(ids, 1), at] + decode(m, slice(128, 256), cols), second, cols)
+            encode(part[side(ids, 1), at] + decode(m, slice(128, 256), cols), second, at)
+            encode(part[side(ids, 1), other], second, other)
 
         over_columns(h, 256, block)
 
@@ -155,46 +153,55 @@
 
 
 def give_kernel(ids, *refs):
-    parts, (m2_up, m2_dn, m3_up, m3_dn, out) = refs[:4], refs[4:]
-    h = m2_up.shape[1]
-    rows = slice(0, 128)
-
-    def f(part):
-        def block(c):
-            cols, far = pl.ds(c, 256), pl.ds(c + h, 256)
-            encode(part[side(ids, 0), cols] + (decode(m3_up, rows, cols) + decode(m2_dn, rows, cols)), out, cols)
-            encode(part[side(ids, 0), far] + (decode(m2_up, rows, cols) + decode(m3_dn, rows, cols)), out, far)
-
-        over_columns(h, 256, block)
-
-    with_part(ids, parts, 0, f)
-
-
-def keep_kernel(ids, *refs):
-    parts, (m2_up, m2_dn, m3_up, m3_dn, x, own, sib) = refs[:4], refs[4:]
+    parts, (m2_up, m2_dn, m3_up, m3_dn, same, cross) = refs[:4], refs[4:]
     h = m2_up.shape[1]
     core = ids[0]
-    start = lax.rem(ids[2] + ids[4], 2) * 128
-
-    def finish(v, at):
-        unit = ids[5] + core * 2 * h + at + lax.broadcasted_iota(I32, (1, 256), 1)
-        mask = (unit < ids[6]).astype(F32)
-        return (0.5 * v * (1 + lax.erf(v * ROOT_HALF)) * mask).astype(BF16)
+    start = lax.rem(ids[2] + ids[4] + 1, 2) * 128
 
     def f(part):
         def block(c):
             cols, far = pl.ds(c, 256), pl.ds(c + h, 256)
-            for out, mine in ((own, core), (sib, 1 - core)):
+            for out, mine in ((same, core), (cross, 1 - core)):
                 rows = pl.ds(pl.multiple_of(mine * 64, 64), 64)
                 base = pl.ds(pl.multiple_of(mine * 64 + start, 64), 64)
-                v = part[base, cols] + (decode(m3_up, rows, cols) + decode(m2_dn, rows, cols)) + decode(x, rows, cols)
-                out[:, cols] = finish(v, c)
-                v = part[base, far] + (decode(m2_up, rows, cols) + decode(m3_dn, rows, cols)) + decode(x, rows, far)
-                out[:, far] = finish(v, c + h)
+                encode(part[base, cols] + (decode(m3_up, rows, cols) + decode(m2_dn, rows, cols)), out, cols)
+                encode(part[base, far] + (decode(m2_up, rows, cols) + decode(m3_dn, rows, cols)), out, far)
 
         over_columns(h, 256, block)
 
     with_part(ids, parts, 0, f)
+
+
+def sum_kernel(ids, *refs):
+    parts, (up, dn, own, sib) = refs[:4], refs[4:]
+    start = lax.rem(ids[2] + ids[4], 2) * 128
+
+    def f(part):
+        def block(c):
+            cols = pl.ds(c, 256)
+            for out, mine in ((own, ids[0]), (sib, 1 - ids[0])):
+                rows = pl.ds(pl.multiple_of(mine * 64, 64), 64)
+                base = pl.ds(pl.multiple_of(mine * 64 + start, 64), 64)
+                out[:, cols] = part[base, cols] + (decode(up, rows, cols) + decode(dn, rows, cols))
+
+        over_columns(own.shape[1], 256, block)
+
+    with_part(ids, parts, 0, f)
+
+
+def keep_kernel(ids, own, sib, x_own, x_sib, out):
+    half = own.shape[1]
+    for v, x, k in ((own, x_own, ids[0]), (sib, x_sib, 1 - ids[0])):
+        def block(c):
+            cols = pl.ds(c, 256)
+            at = k * half + c
+            hidden = v[:, cols] + decode(x, slice(0, 64), cols)
+            unit = ids[5] + at + lax.broadcasted_iota(I32, (1, 256), 1)
+            mask = (unit < ids[6]).astype(F32)
+            act = 0.5 * hidden * (1 + lax.erf(hidden * ROOT_HALF)) * mask
+            out[:, pl.ds(pl.multiple_of(at, 256), 256)] = act.astype(BF16)
+
+        over_columns(half, 256, block)
 
 
 def earlier_kernel(ids, p0, p1, p2, p3, out, std):
@@ -212,13 +219,15 @@
             out[:, i * 128:(i + 1) * 128] = jnp.concatenate([own, sib], axis=0).T
 
 
-def grad_kernel(ids, *refs):
-    own, sib, p_t, out, rhs = refs[:8], refs[8:16], refs[16], refs[17], refs[18]
+def grad_kernel(base, ids, *refs):
+    near, p_t, out, rhs = refs[:16], refs[16], refs[-2], refs[-1]
+    own = near[:3] + near[12:13] + near[3:6] + near[13:14]
+    sib = near[6:9] + near[14:15] + near[9:12] + near[15:16]
     for j in range(8):
         rhs[j * 128:j * 128 + 64, :] = own[j][...]
         rhs[j * 128 + 64:j * 128 + 128, :] = sib[j][...]
     tn = out.shape[1]
-    unit = ids[5] + pl.program_id(0) * tn + lax.broadcasted_iota(I32, (1, tn), 1)
+    unit = ids[5] + (pl.program_id(0) + base) * tn + lax.broadcasted_iota(I32, (1, tn), 1)
     mask = (unit < ids[6]).astype(F32)
     grad = jnp.dot(p_t[...], rhs[...], preferred_element_type=F32)
     out[...] = (grad * mask).astype(BF16)
@@ -235,7 +244,7 @@
     core = col % 2
     ids = jnp.stack([core, (col // 2) % 4, col // 8, row % 4, row // 4, row * units, active_blocks[0] * BLOCK, 0]).astype(I32)
 
-    def call(f, outs, grid=(), specs=None, out_specs=None, scratch=(), flops=1 << 20, limit=16):
+    def call(f, outs, grid=(), specs=None, out_specs=None, scratch=(), flops=1 << 20, limit=8):
         params = pltpu.CompilerParams(vmem_limit_bytes=limit << 20)
         cost = pl.CostEstimate(flops=flops, bytes_accessed=1 << 20, transcendentals=0)
         spec = pltpu.PrefetchScalarGridSpec(num_scalar_prefetch=1, grid=grid, in_specs=specs, out_specs=out_specs, scratch_shapes=scratch)
@@ -257,9 +266,15 @@
     t_sib = [send(a, SIB) for a in t_own]
     w_sib = send(weight, SIB)
 
-    h_own = [hidden_grad, send(hidden_grad, YUP), send(hidden_grad, YDN), send(hidden_grad, YTWO)]
-    h_own = h_own + [send(a, XLO) for a in h_own]
-    h_sib = [send(a, SIB) for a in h_own]
+    h_near = [hidden_grad, send(hidden_grad, YUP), send(hidden_grad, YDN)]
+    h_left = send(h_near[1][:, :half], YUP)
+    h_right = send(h_near[2][:, half:], YDN)
+    far = lambda a: send(a, XLO)
+    h_near = h_near + [far(a) for a in h_near]
+    h_left, h_right = [h_left, far(h_left)], [h_right, far(h_right)]
+    s_near = [send(a, SIB) for a in h_near]
+    s_left = [send(a, SIB) for a in h_left]
+    s_right = [send(a, SIB) for a in h_right]
 
     p_own = gather_row(prev_tokens)
 
@@ -268,7 +283,11 @@
     quarter = half // 2
     hbm = pl.BlockSpec(memory_space=pltpu.HBM)
     w_half = V((slab, half), BF16)
-    w_own, w_far = call(load_kernel, [w_half] * 2, (), [hbm] * 2, [vmem()] * 2, [pltpu.SemaphoreType.DMA((2,))])(weight, w_sib)
+
+    def load(w, limit):
+        return call(load_kernel, [w_half], (), [hbm], [vmem()], [pltpu.SemaphoreType.DMA((1,))], limit=limit)(w)[0]
+
+    w_own, w_far = load(weight, 50), load(w_sib, 46)
 
     def partials(which):
         n = len(which)
@@ -282,28 +301,38 @@
     msg, piece = V((256 + TAG, quarter), I16), V((128 + TAG, quarter), I16)
     m1_up, m1_dn = small(first_kernel, [msg] * 2, *parts)
     m1_up, m1_dn = send(m1_up, YUP), send(m1_dn, YDN)
-    up1, up2, dn1, dn2 = small(second_kernel, [piece] * 4, *parts)
-    m2_up1, m2_dn1 = send(up1, YUP), send(dn1, YDN)
-    m2_up2, m2_dn2 = send(up2, YUP), send(dn2, YDN)
-    m3_up1, m3_up2 = small(partial(relay_kernel, 1), [piece] * 2, *parts, m1_up)
-    m3_dn1, m3_dn2 = small(partial(relay_kernel, -1), [piece] * 2, *parts, m1_dn)
-    m3_up1, m3_dn1 = send(m3_up1, YUP), send(m3_dn1, YDN)
-    m3_up2, m3_dn2 = send(m3_up2, YUP), send(m3_dn2, YDN)
-    given, = small(give_kernel, [V((128 + TAG, half), I16)], *parts, m2_up1, m2_dn1, m3_up1, m3_dn1)
-    x_in = send(given, XLO)
-    act = V((64, half), BF16)
-    act_own, act_give = small(keep_kernel, [act] * 2, *parts, m2_up2, m2_dn2, m3_up2, m3_dn2, x_in)
-    act_sib = send(act_give, SIB)
-    activation = jnp.where(core == 0, jnp.concatenate([act_own, act_sib], 1), jnp.concatenate([act_sib, act_own], 1))
+    m2_up, m2_dn = small(second_kernel, [piece] * 2, *parts)
+    m2_up, m2_dn = send(m2_up, YUP), send(m2_dn, YDN)
+    wide = V((128 + TAG, half), I16)
+    m3_up, m4_up = small(partial(relay_kernel, 1), [piece, wide], *parts, m1_up)
+    m3_dn, m4_dn = small(partial(relay_kernel, -1), [piece, wide], *parts, m1_dn)
+    m3_up, m3_dn = send(m3_up, YUP), send(m3_dn, YDN)
+    m4_up, m4_dn = send(m4_up, YUP), send(m4_dn, YDN)
+    same, cross = small(give_kernel, [V((64 + TAG, half), I16)] * 2, *parts, m2_up, m2_dn, m3_up, m3_dn)
+    x_own, x_sib = send(same, XLO), send(cross, XLO_SIB)
+    kept, other = small(sum_kernel, [V((64, half), F32)] * 2, *parts, m4_up, m4_dn)
+    other = send(other, SIB)
+    activation, = small(keep_kernel, [S((64, units), BF16)], kept, other, x_own, x_sib)
 
     p_t, = call(earlier_kernel, [V((slab, 1024), BF16)], (), [vmem()] * 4, [vmem()], [V((1024, slab), BF16)])(*p_own)
     tg = 1024
-    weight_grad = call(
-        grad_kernel, S((slab, units), BF16), (units // tg,),
-        [pl.BlockSpec((64, tg), lambda i, s: (0, i))] * 16 + [vmem()],
-        pl.BlockSpec((slab, tg), lambda i, s: (0, i)), [V((1024, tg), BF16)],
-        flops=2 * 1024 * slab * units, limit=24,
-    )(*h_own, *h_sib, p_t)
+    steps = units // tg // 2
+
+    def grad(base, far, *before):
+        return pl.pallas_call(
+            partial(grad_kernel, base), out_shape=S((slab, units), BF16),
+            grid_spec=pltpu.PrefetchScalarGridSpec(
+                num_scalar_prefetch=1, grid=(steps,),
+                in_specs=[pl.BlockSpec((64, tg), lambda i, s: (0, i + base))] * 12 + [pl.BlockSpec((64, tg), lambda i, s: (0, i))] * 4
+                + [vmem()] + [pl.BlockSpec(memory_space=pl.ANY)] * len(before),
+                out_specs=pl.BlockSpec((slab, tg), lambda i, s: (0, i + base)), scratch_shapes=[V((1024, tg), BF16)],
+            ),
+            compiler_params=pltpu.CompilerParams(vmem_limit_bytes=24 << 20),
+            cost_estimate=pl.CostEstimate(flops=1024 * slab * units, bytes_accessed=1 << 20, transcendentals=0),
+            input_output_aliases={18: 0} if before else {},
+        )(ids, *h_near, *s_near, *far, p_t, *before)
+
+    weight_grad = grad(steps, h_right + s_right, grad(0, h_left + s_left))
     return (activation, weight_grad)
 
 

time: 232 us -> 176 us (0.76)
  the two profiles are of different devices: /device:TPU:0 before, /device:TPU:97 now
where the time goes in v2:
time: 176 us
  waiting for transfers between devices  71.7 us (41%)
  starting transfers between devices  52.9 us (30%)
  Pallas kernels  47.3 us (27%)
  other arithmetic  1.93 us (1%)
    ppermute x43, waiting for transfers between devices, send(): return lax.ppermute(a, ('row', 'col'), p)  71.7 us
    ppermute x43, starting transfers between devices, send(): return lax.ppermute(a, ('row', 'col'), p)  52.9 us
    pallas_call x13, Pallas kernels, run(): return g(ids, *args)  31.6 us
    pallas_call x2, Pallas kernels, grad(): pl.pallas_call(partial(grad_kernel, base), out_shape=S((slab, units), BF1...  15.6 us
  transfers between devices with their start and end apart: 43, of which 12 were waited for; matrix products, arithmetic and copies ran while one was open for 1% of the time, Pallas kernels for 26%

profile of v2, /device:TPU:97, one launch (start us, length us, event | category | flops | bytes accessed | tf_op | source)
XLA Modules:
  0.0 176.1 jit_solution(4380645185005825482)
XLA Ops:
  1.4 2.7 %collective-permute-start.21 = (bf16[64,6144]{1,0:T(8,128)(2,1)}, bf16[64,6144]{1,0:T(8,128)(2,1)S(1)}, u32[]{:S(2)}, u32[]{:S(2)}) collective-permute-start(bf16[64,6144]{1,0:T(8,128)(2,1)} %refs_0_.3), channel_id=1, source_target_pairs={{0,6},{1,7},{2,0},{3,1},{4,2},{5,3},{6,4},{7,5},{8,14},{9,15},{10,... | collective-permute-start | bytes 2359304 | tf_op jit(solution)/shard_map/ppermute | solution.py:38
  4.1 2.7 %collective-permute-start = (bf16[128,768]{1,0:T(8,128)(2,1)}, bf16[128,768]{1,0:T(8,128)(2,1)S(1)}, u32[]{:S(2)}, u32[]{:S(2)}) collective-permute-start(bf16[128,768]{1,0:T(8,128)(2,1)} %param.5), channel_id=1, source_target_pairs={{0,64},{1,65},{2,66},{3,67},{4,68},{5,69},{6,70},{7,71},{8,72},{9,... | collective-permute-start | bytes 589832 | tf_op jit(solution)/shard_map/ppermute | solution.py:38
  6.9 5.1 %collective-permute-done = bf16[128,768]{1,0:T(8,128)(2,1)S(1)} collective-permute-done((bf16[128,768]{1,0:T(8,128)(2,1)}, bf16[128,768]{1,0:T(8,128)(2,1)S(1)}, u32[]{:S(2)}, u32[]{:S(2)}) %collective-permute-start) | collective-permute-done | bytes 196640 | tf_op jit(solution)/shard_map/ppermute | solution.py:38
  13.2 2.7 %collective-permute-start.35 = (bf16[128,768]{1,0:T(8,128)(2,1)}, bf16[128,768]{1,0:T(8,128)(2,1)S(1)}, u32[]{:S(2)}, u32[]{:S(2)}) collective-permute-start(bf16[128,768]{1,0:T(8,128)(2,1)} %param.6), channel_id=1, source_target_pairs={{0,64},{1,65},{2,66},{3,67},{4,68},{5,69},{6,70},{7,71},{8,72},{9,... | collective-permute-start | bytes 589832 | tf_op jit(solution)/shard_map/ppermute | solution.py:38
  24.1 3.4 %collective-permute-start.8 = (bf16[2,128,768]{2,1,0:T(8,128)(2,1)S(1)}, bf16[2,128,768]{2,1,0:T(8,128)(2,1)S(1)}, u32[]{:S(2)}, u32[]{:S(2)}) collective-permute-start(bf16[2,128,768]{2,1,0:T(8,128)(2,1)S(1)} %collective-permute-done.7.refs_0_), channel_id=1, source_target_pairs={{0,1},{1,0},{2,3},{3,2},{4,5},{5,4},{6,7},{7,6},{8,9},{9,8},{10,11... | collective-permute-start | bytes 1179656 | tf_op jit(solution)/shard_map/ppermute | solution.py:38
  28.7 3.1 %shard_map.68.refs_2_.refs_4_ = bf16[768,3072]{1,0:T(8,128)(2,1)S(1)} custom-call(s32[8]{0:T(128)} %stack.46.ids, bf16[768,6144]{1,0:T(8,128)(2,1)} %w.1), custom_call_target="tpu_custom_call" | custom-call | flops 1048576 | bytes 1048576 | tf_op jit(solution)/shard_map/pallas_call | solution.py:254
  32.9 2.9 %shard_map.69.refs_3_.refs_5_ = bf16[768,3072]{1,0:T(8,128)(2,1)S(1)} custom-call(s32[8]{0:T(128)S(1)} %copy-done.1, bf16[768,6144]{1,0:T(8,128)(2,1)} %collective-permute-done.2.w), custom_call_target="tpu_custom_call" | custom-call | flops 1048576 | bytes 1048576 | tf_op jit(solution)/shard_map/pallas_call | solution.py:254
  39.5 3.2 %shard_map.70.refs_0_ = f32[256,3072]{1,0:T(8,128)S(1)} custom-call(s32[8]{0:T(128)S(1)} %copy-done.1, bf16[2,128,768]{2,1,0:T(8,128)(2,1)S(1)} %pad_maximum_fusion.refs_0_, bf16[2,128,768]{2,1,0:T(8,128)(2,1)S(1)} %collective-permute-done.1.refs_1_, bf16[768,3072]{1,0:T(8,128)(2,1)S(1)} %shard_map.68.refs_2_.refs_4_, ...), custom_call_target="tpu_custom_call" | custom-call | flops 2415919104 | bytes 1048576 | tf_op jit(solution)/shard_map/pallas_call | solution.py:254
  42.7 3.2 %shard_map.72.refs_3_ = f32[256,3072]{1,0:T(8,128)S(1)} custom-call(s32[8]{0:T(128)S(1)} %copy-done.1, bf16[2,128,768]{2,1,0:T(8,128)(2,1)S(1)} %collective-permute-done.7.refs_0_, bf16[2,128,768]{2,1,0:T(8,128)(2,1)S(1)} %collective-permute-done.8.refs_1_, bf16[768,3072]{1,0:T(8,128)(2,1)S(1)} %shard_map.68.refs_2_.refs_4_, ...), custom_call_target="tpu_custom_call" | custom-call | flops 2415919104 | bytes 1048576 | tf_op jit(solution)/shard_map/pallas_call | solution.py:254
  48.7 3.9 %collective-permute-start.38 = (bf16[2,128,768]{2,1,0:T(8,128)(2,1)S(1)}, bf16[2,128,768]{2,1,0:T(8,128)(2,1)S(1)}, u32[]{:S(2)}, u32[]{:S(2)}) collective-permute-start(bf16[2,128,768]{2,1,0:T(8,128)(2,1)S(1)} %pad_maximum_fusion.1.p0), channel_id=1, source_target_pairs={{0,32},{1,33},{2,34},{3,35},{4,36},{5,37},{6,38},{7,39},{8,40},{9,... | collective-permute-start | bytes 1179656 | tf_op jit(solution)/shard_map/ppermute | solution.py:38
  52.9 6.7 %shard_map.71 = (f32[256,3072]{1,0:T(8,128)S(1)}, f32[256,3072]{1,0:T(8,128)S(1)}) custom-call(s32[8]{0:T(128)S(1)} %copy-done.1, bf16[2,128,768]{2,1,0:T(8,128)(2,1)} %collective-permute-done.3.refs_0_, bf16[2,128,768]{2,1,0:T(8,128)(2,1)} %collective-permute-done.4.refs_1_, bf16[2,128,768]{2,1,0:T(8,128)(2,1)S(1)} %collective-permute-done.5.refs_2_, ...), custom_call_target="tpu_custom_call" | custom-call | flops 4831838208 | bytes 1048576 | tf_op jit(solution)/shard_map/pallas_call | solution.py:254
  60.6 2.8 %collective-permute-start.31 = (bf16[64,3072]{1,0:T(8,128)(2,1)S(1)}, bf16[64,3072]{1,0:T(8,128)(2,1)S(1)}, u32[]{:S(2)}, u32[]{:S(2)}) collective-permute-start(bf16[64,3072]{1,0:T(8,128)(2,1)S(1)} %slice.8), channel_id=1, source_target_pairs={{0,6},{1,7},{2,0},{3,1},{4,2},{5,3},{6,4},{7,5},{8,14},{9,15},{10,... | collective-permute-start | bytes 1179656 | tf_op jit(solution)/shard_map/ppermute | solution.py:38
  65.1 5.2 %collective-permute-done.38.p3 = bf16[2,128,768]{2,1,0:T(8,128)(2,1)S(1)} collective-permute-done((bf16[2,128,768]{2,1,0:T(8,128)(2,1)S(1)}, bf16[2,128,768]{2,1,0:T(8,128)(2,1)S(1)}, u32[]{:S(2)}, u32[]{:S(2)}) %collective-permute-start.38) | collective-permute-done | bytes 393248 | tf_op jit(solution)/shard_map/ppermute | solution.py:38
  73.4 25.3 %collective-permute-done.39.refs_12_ = bf16[64,3072]{1,0:T(8,128)(2,1)S(1)} collective-permute-done((bf16[64,3072]{1,0:T(8,128)(2,1)S(1)}, bf16[64,3072]{1,0:T(8,128)(2,1)S(1)}, u32[]{:S(2)}, u32[]{:S(2)}) %collective-permute-start.39) | collective-permute-done | bytes 393248 | tf_op jit(solution)/shard_map/ppermute | solution.py:38
  104.0 2.7 %collective-permute-start.12 = (s16[136,3072]{1,0:T(8,128)(2,1)S(1)}, s16[136,3072]{1,0:T(8,128)(2,1)S(1)}, u32[]{:S(2)}, u32[]{:S(2)}) collective-permute-start(s16[136,3072]{1,0:T(8,128)(2,1)S(1)} %get-tuple-element.21), channel_id=1, source_target_pairs={{0,6},{1,7},{2,0},{3,1},{4,2},{5,3},{6,4},{7,5},{8,14},{9,15},{10,... | collective-permute-start | bytes 2506760 | tf_op jit(solution)/shard_map/ppermute | solution.py:38
  109.4 7.3 %collective-permute-done.32.refs_13_ = bf16[64,3072]{1,0:T(8,128)(2,1)S(1)} collective-permute-done((bf16[64,3072]{1,0:T(8,128)(2,1)S(1)}, bf16[64,3072]{1,0:T(8,128)(2,1)S(1)}, u32[]{:S(2)}, u32[]{:S(2)}) %collective-permute-start.32) | collective-permute-done | bytes 393248 | tf_op jit(solution)/shard_map/ppermute | solution.py:38
  116.8 2.6 %collective-permute-start.29 = (bf16[64,6144]{1,0:T(8,128)(2,1)S(1)}, bf16[64,6144]{1,0:T(8,128)(2,1)S(1)}, u32[]{:S(2)}, u32[]{:S(2)}) collective-permute-start(bf16[64,6144]{1,0:T(8,128)(2,1)S(1)} %collective-permute-done.23.refs_4_), channel_id=1, source_target_pairs={{0,1},{1,0},{2,3},{3,2},{4,5},{5,4},{6,7},{7,6},{8,9},{9,8},{10,11... | collective-permute-start | bytes 2359304 | tf_op jit(solution)/shard_map/ppermute | solution.py:38
  119.4 5.8 %collective-permute-done.40.refs_13_ = bf16[64,3072]{1,0:T(8,128)(2,1)S(1)} collective-permute-done((bf16[64,3072]{1,0:T(8,128)(2,1)S(1)}, bf16[64,3072]{1,0:T(8,128)(2,1)S(1)}, u32[]{:S(2)}, u32[]{:S(2)}) %collective-permute-start.40) | collective-permute-done | bytes 393248 | tf_op jit(solution)/shard_map/ppermute | solution.py:38
  128.3 2.7 %collective-permute-start.15 = (s16[136,1536]{1,0:T(8,128)(2,1)S(1)}, s16[136,1536]{1,0:T(8,128)(2,1)S(1)}, u32[]{:S(2)}, u32[]{:S(2)}) collective-permute-start(s16[136,1536]{1,0:T(8,128)(2,1)S(1)} %get-tuple-element.25), channel_id=1, source_target_pairs={{0,6},{1,7},{2,0},{3,1},{4,2},{5,3},{6,4},{7,5},{8,14},{9,15},{10,... | collective-permute-start | bytes 1253384 | tf_op jit(solution)/shard_map/ppermute | solution.py:38
  134.7 6.0 %collective-permute-done.14.refs_4_ = s16[136,1536]{1,0:T(8,128)(2,1)S(1)} collective-permute-done((s16[136,1536]{1,0:T(8,128)(2,1)S(1)}, s16[136,1536]{1,0:T(8,128)(2,1)S(1)}, u32[]{:S(2)}, u32[]{:S(2)}) %collective-permute-start.14) | collective-permute-done | bytes 417824 | tf_op jit(solution)/shard_map/ppermute | solution.py:38
  142.0 7.8 %shard_map.81.refs_17_ = bf16[768,6144]{1,0:T(8,128)(2,1)} custom-call(s32[8]{0:T(128)S(1)} %copy-done.1, bf16[64,6144]{1,0:T(8,128)(2,1)S(1)} %copy-done, bf16[64,6144]{1,0:T(8,128)(2,1)S(1)} %collective-permute-done.20.refs_1_, bf16[64,6144]{1,0:T(8,128)(2,1)S(1)} %collective-permute-done.21.refs_2_, bf16[64,6144]{1,0:T(8,128)(2,1)S(1)} %collective-permute-done.22.refs_3_, ...), custom_call_target="tpu_custom_call" | custom-call | flops 4831838208 | bytes 1048576 | tf_op jit(solution)/shard_map/pallas_call | solution.py:322
  152.6 3.6 %collective-permute-start.19 = (s16[72,3072]{1,0:T(8,128)(2,1)S(1)}, s16[72,3072]{1,0:T(8,128)(2,1)S(1)}, u32[]{:S(2)}, u32[]{:S(2)}) collective-permute-start(s16[72,3072]{1,0:T(8,128)(2,1)S(1)} %get-tuple-element.29), channel_id=1, source_target_pairs={{0,9},{1,8},{2,11},{3,10},{4,13},{5,12},{6,15},{7,14},{8,1},{9,0},... | collective-permute-start | bytes 1327112 | tf_op jit(solution)/shard_map/ppermute | solution.py:38
  156.2 7.8 %shard_map.82 = bf16[768,6144]{1,0:T(8,128)(2,1)} custom-call(s32[8]{0:T(128)S(1)} %copy-done.1, bf16[64,6144]{1,0:T(8,128)(2,1)S(1)} %copy-done, bf16[64,6144]{1,0:T(8,128)(2,1)S(1)} %collective-permute-done.20.refs_1_, bf16[64,6144]{1,0:T(8,128)(2,1)S(1)} %collective-permute-done.21.refs_2_, ...), custom_call_target="tpu_custom_call", output_to_operand_aliasing={{}: (18, {})} | custom-call | flops 4831838208 | bytes 1048576 | tf_op jit(solution)/shard_map/pallas_call | solution.py:322
  164.0 9.7 %collective-permute-done.19.x_sib = s16[72,3072]{1,0:T(8,128)(2,1)S(1)} collective-permute-done((s16[72,3072]{1,0:T(8,128)(2,1)S(1)}, s16[72,3072]{1,0:T(8,128)(2,1)S(1)}, u32[]{:S(2)}, u32[]{:S(2)}) %collective-permute-start.19) | collective-permute-done | bytes 442400 | tf_op jit(solution)/shard_map/ppermute | solution.py:38
  (90 shorter events, 45.4 us)
Async XLA Ops:
  0.6 26.8 %collective-permute-start.2 = (bf16[768,6144]{1,0:T(8,128)(2,1)}, bf16[768,6144]{1,0:T(8,128)(2,1)}, u32[]{:S(2)}, u32[]{:S(2)}) collective-permute-start(bf16[768,6144]{1,0:T(8,128)(2,1)} %w.1), channel_id=1, source_target_pairs={{0,1},{1,0},{2,3},{3,2},{4,5},{5,4},{6,7},{7,6},{8,9},{9,8},{10,11... | collective-permute-start | bytes 28311560 | tf_op jit(solution)/shard_map/ppermute | solution.py:38
  1.4 22.7 %collective-permute-start.21 = (bf16[64,6144]{1,0:T(8,128)(2,1)}, bf16[64,6144]{1,0:T(8,128)(2,1)S(1)}, u32[]{:S(2)}, u32[]{:S(2)}) collective-permute-start(bf16[64,6144]{1,0:T(8,128)(2,1)} %refs_0_.3), channel_id=1, source_target_pairs={{0,6},{1,7},{2,0},{3,1},{4,2},{5,3},{6,4},{7,5},{8,14},{9,15},{10,... | collective-permute-start | bytes 2359304 | tf_op jit(solution)/shard_map/ppermute | solution.py:38
  16.0 19.8 %collective-permute-start.1 = (bf16[2,128,768]{2,1,0:T(8,128)(2,1)S(1)}, bf16[2,128,768]{2,1,0:T(8,128)(2,1)S(1)}, u32[]{:S(2)}, u32[]{:S(2)}) collective-permute-start(bf16[2,128,768]{2,1,0:T(8,128)(2,1)S(1)} %pad_maximum_fusion.refs_0_), channel_id=1, source_target_pairs={{0,1},{1,0},{2,3},{3,2},{4,5},{5,4},{6,7},{7,6},{8,9},{9,8},{10,11... | collective-permute-start | bytes 1179656 | tf_op jit(solution)/shard_map/ppermute | solution.py:38
  19.9 17.2 %collective-permute-start.3 = (bf16[2,128,768]{2,1,0:T(8,128)(2,1)S(1)}, bf16[2,128,768]{2,1,0:T(8,128)(2,1)}, u32[]{:S(2)}, u32[]{:S(2)}) collective-permute-start(bf16[2,128,768]{2,1,0:T(8,128)(2,1)S(1)} %pad_maximum_fusion.refs_0_), channel_id=1, source_target_pairs={{0,16},{1,17},{2,18},{3,19},{4,20},{5,21},{6,22},{7,23},{8,24},{9,... | collective-permute-start | bytes 1179656 | tf_op jit(solution)/shard_map/ppermute | solution.py:38
  24.1 15.3 %collective-permute-start.8 = (bf16[2,128,768]{2,1,0:T(8,128)(2,1)S(1)}, bf16[2,128,768]{2,1,0:T(8,128)(2,1)S(1)}, u32[]{:S(2)}, u32[]{:S(2)}) collective-permute-start(bf16[2,128,768]{2,1,0:T(8,128)(2,1)S(1)} %collective-permute-done.7.refs_0_), channel_id=1, source_target_pairs={{0,1},{1,0},{2,3},{3,2},{4,5},{5,4},{6,7},{7,6},{8,9},{9,8},{10,11... | collective-permute-start | bytes 1179656 | tf_op jit(solution)/shard_map/ppermute | solution.py:38
  27.4 21.3 %collective-permute-start.20 = (bf16[64,6144]{1,0:T(8,128)(2,1)}, bf16[64,6144]{1,0:T(8,128)(2,1)S(1)}, u32[]{:S(2)}, u32[]{:S(2)}) collective-permute-start(bf16[64,6144]{1,0:T(8,128)(2,1)} %refs_0_.3), channel_id=1, source_target_pairs={{0,2},{1,3},{2,4},{3,5},{4,6},{5,7},{6,0},{7,1},{8,10},{9,11},{10,... | collective-permute-start | bytes 2359304 | tf_op jit(solution)/shard_map/ppermute | solution.py:38
  35.9 34.5 %collective-permute-start.22 = (bf16[64,6144]{1,0:T(8,128)(2,1)S(1)}, bf16[64,6144]{1,0:T(8,128)(2,1)S(1)}, u32[]{:S(2)}, u32[]{:S(2)}) collective-permute-start(bf16[64,6144]{1,0:T(8,128)(2,1)S(1)} %copy-done), channel_id=1, source_target_pairs={{0,8},{1,9},{2,10},{3,11},{4,12},{5,13},{6,14},{7,15},{8,0},{9,1},... | collective-permute-start | bytes 2359304 | tf_op jit(solution)/shard_map/ppermute | solution.py:38
  47.4 24.3 %collective-permute-start.25 = (bf16[64,6144]{1,0:T(8,128)(2,1)S(1)}, bf16[64,6144]{1,0:T(8,128)(2,1)S(1)}, u32[]{:S(2)}, u32[]{:S(2)}) collective-permute-start(bf16[64,6144]{1,0:T(8,128)(2,1)S(1)} %copy-done), channel_id=1, source_target_pairs={{0,1},{1,0},{2,3},{3,2},{4,5},{5,4},{6,7},{7,6},{8,9},{9,8},{10,11... | collective-permute-start | bytes 2359304 | tf_op jit(solution)/shard_map/ppermute | solution.py:38
  48.7 21.6 %collective-permute-start.38 = (bf16[2,128,768]{2,1,0:T(8,128)(2,1)S(1)}, bf16[2,128,768]{2,1,0:T(8,128)(2,1)S(1)}, u32[]{:S(2)}, u32[]{:S(2)}) collective-permute-start(bf16[2,128,768]{2,1,0:T(8,128)(2,1)S(1)} %pad_maximum_fusion.1.p0), channel_id=1, source_target_pairs={{0,32},{1,33},{2,34},{3,35},{4,36},{5,37},{6,38},{7,39},{8,40},{9,... | collective-permute-start | bytes 1179656 | tf_op jit(solution)/shard_map/ppermute | solution.py:38
  52.6 47.7 %collective-permute-start.23 = (bf16[64,6144]{1,0:T(8,128)(2,1)S(1)}, bf16[64,6144]{1,0:T(8,128)(2,1)S(1)}, u32[]{:S(2)}, u32[]{:S(2)}) collective-permute-start(bf16[64,6144]{1,0:T(8,128)(2,1)S(1)} %collective-permute-done.20.refs_1_), channel_id=1, source_target_pairs={{0,8},{1,9},{2,10},{3,11},{4,12},{5,13},{6,14},{7,15},{8,0},{9,1},... | collective-permute-start | bytes 2359304 | tf_op jit(solution)/shard_map/ppermute | solution.py:38
  70.2 30.1 %collective-permute-start.9 = (s16[264,1536]{1,0:T(8,128)(2,1)S(1)}, s16[264,1536]{1,0:T(8,128)(2,1)S(1)}, u32[]{:S(2)}, u32[]{:S(2)}) collective-permute-start(s16[264,1536]{1,0:T(8,128)(2,1)S(1)} %get-tuple-element.18), channel_id=1, source_target_pairs={{0,2},{1,3},{2,4},{3,5},{4,6},{5,7},{6,0},{7,1},{8,10},{9,11},{10,... | collective-permute-start | bytes 2433032 | tf_op jit(solution)/shard_map/ppermute | solution.py:38
  70.3 28.3 %collective-permute-start.39 = (bf16[64,3072]{1,0:T(8,128)(2,1)S(1)}, bf16[64,3072]{1,0:T(8,128)(2,1)S(1)}, u32[]{:S(2)}, u32[]{:S(2)}) collective-permute-start(bf16[64,3072]{1,0:T(8,128)(2,1)S(1)} %slice.9), channel_id=1, source_target_pairs={{0,2},{1,3},{2,4},{3,5},{4,6},{5,7},{6,0},{7,1},{8,10},{9,11},{10,... | collective-permute-start | bytes 1179656 | tf_op jit(solution)/shard_map/ppermute | solution.py:38
  71.7 30.7 %collective-permute-start.11 = (s16[264,1536]{1,0:T(8,128)(2,1)S(1)}, s16[264,1536]{1,0:T(8,128)(2,1)S(1)}, u32[]{:S(2)}, u32[]{:S(2)}) collective-permute-start(s16[264,1536]{1,0:T(8,128)(2,1)S(1)} %get-tuple-element.20), channel_id=1, source_target_pairs={{0,6},{1,7},{2,0},{3,1},{4,2},{5,3},{6,4},{7,5},{8,14},{9,15},{10,... | collective-permute-start | bytes 2433032 | tf_op jit(solution)/shard_map/ppermute | solution.py:38
  73.1 30.9 %collective-permute-start.24 = (bf16[64,6144]{1,0:T(8,128)(2,1)S(1)}, bf16[64,6144]{1,0:T(8,128)(2,1)S(1)}, u32[]{:S(2)}, u32[]{:S(2)}) collective-permute-start(bf16[64,6144]{1,0:T(8,128)(2,1)S(1)} %collective-permute-done.21.refs_2_), channel_id=1, source_target_pairs={{0,8},{1,9},{2,10},{3,11},{4,12},{5,13},{6,14},{7,15},{8,0},{9,1},... | collective-permute-start | bytes 2359304 | tf_op jit(solution)/shard_map/ppermute | solution.py:38
  102.4 25.9 %collective-permute-start.10 = (s16[136,3072]{1,0:T(8,128)(2,1)S(1)}, s16[136,3072]{1,0:T(8,128)(2,1)S(1)}, u32[]{:S(2)}, u32[]{:S(2)}) collective-permute-start(s16[136,3072]{1,0:T(8,128)(2,1)S(1)} %get-tuple-element.19), channel_id=1, source_target_pairs={{0,2},{1,3},{2,4},{3,5},{4,6},{5,7},{6,0},{7,1},{8,10},{9,11},{10,... | collective-permute-start | bytes 2506760 | tf_op jit(solution)/shard_map/ppermute | solution.py:38
  104.0 27.0 %collective-permute-start.12 = (s16[136,3072]{1,0:T(8,128)(2,1)S(1)}, s16[136,3072]{1,0:T(8,128)(2,1)S(1)}, u32[]{:S(2)}, u32[]{:S(2)}) collective-permute-start(s16[136,3072]{1,0:T(8,128)(2,1)S(1)} %get-tuple-element.21), channel_id=1, source_target_pairs={{0,6},{1,7},{2,0},{3,1},{4,2},{5,3},{6,4},{7,5},{8,14},{9,15},{10,... | collective-permute-start | bytes 2506760 | tf_op jit(solution)/shard_map/ppermute | solution.py:38
  107.0 18.2 %collective-permute-start.40 = (bf16[64,3072]{1,0:T(8,128)(2,1)S(1)}, bf16[64,3072]{1,0:T(8,128)(2,1)S(1)}, u32[]{:S(2)}, u32[]{:S(2)}) collective-permute-start(bf16[64,3072]{1,0:T(8,128)(2,1)S(1)} %collective-permute-done.39.refs_12_), channel_id=1, source_target_pairs={{0,8},{1,9},{2,10},{3,11},{4,12},{5,13},{6,14},{7,15},{8,0},{9,1},... | collective-permute-start | bytes 1179656 | tf_op jit(solution)/shard_map/ppermute | solution.py:38
  108.2 20.0 %collective-permute-start.41 = (bf16[64,3072]{1,0:T(8,128)(2,1)S(1)}, bf16[64,3072]{1,0:T(8,128)(2,1)S(1)}, u32[]{:S(2)}, u32[]{:S(2)}) collective-permute-start(bf16[64,3072]{1,0:T(8,128)(2,1)S(1)} %collective-permute-done.39.refs_12_), channel_id=1, source_target_pairs={{0,1},{1,0},{2,3},{3,2},{4,5},{5,4},{6,7},{7,6},{8,9},{9,8},{10,11... | collective-permute-start | bytes 1179656 | tf_op jit(solution)/shard_map/ppermute | solution.py:38
  116.8 17.4 %collective-permute-start.29 = (bf16[64,6144]{1,0:T(8,128)(2,1)S(1)}, bf16[64,6144]{1,0:T(8,128)(2,1)S(1)}, u32[]{:S(2)}, u32[]{:S(2)}) collective-permute-start(bf16[64,6144]{1,0:T(8,128)(2,1)S(1)} %collective-permute-done.23.refs_4_), channel_id=1, source_target_pairs={{0,1},{1,0},{2,3},{3,2},{4,5},{5,4},{6,7},{7,6},{8,9},{9,8},{10,11... | collective-permute-start | bytes 2359304 | tf_op jit(solution)/shard_map/ppermute | solution.py:38
  133.9 22.3 %collective-permute-start.33 = (bf16[64,3072]{1,0:T(8,128)(2,1)S(1)}, bf16[64,3072]{1,0:T(8,128)(2,1)S(1)}, u32[]{:S(2)}, u32[]{:S(2)}) collective-permute-start(bf16[64,3072]{1,0:T(8,128)(2,1)S(1)} %collective-permute-done.31.refs_12_), channel_id=1, source_target_pairs={{0,1},{1,0},{2,3},{3,2},{4,5},{5,4},{6,7},{7,6},{8,9},{9,8},{10,11... | collective-permute-start | bytes 1179656 | tf_op jit(solution)/shard_map/ppermute | solution.py:38
  134.2 22.0 %collective-permute-start.34 = (bf16[64,3072]{1,0:T(8,128)(2,1)S(1)}, bf16[64,3072]{1,0:T(8,128)(2,1)S(1)}, u32[]{:S(2)}, u32[]{:S(2)}) collective-permute-start(bf16[64,3072]{1,0:T(8,128)(2,1)S(1)} %collective-permute-done.32.refs_13_), channel_id=1, source_target_pairs={{0,1},{1,0},{2,3},{3,2},{4,5},{5,4},{6,7},{7,6},{8,9},{9,8},{10,11... | collective-permute-start | bytes 1179656 | tf_op jit(solution)/shard_map/ppermute | solution.py:38
  134.7 15.2 %collective-permute-start.16 = (s16[136,1536]{1,0:T(8,128)(2,1)S(1)}, s16[136,1536]{1,0:T(8,128)(2,1)S(1)}, u32[]{:S(2)}, u32[]{:S(2)}) collective-permute-start(s16[136,1536]{1,0:T(8,128)(2,1)S(1)} %get-tuple-element.26), channel_id=1, source_target_pairs={{0,2},{1,3},{2,4},{3,5},{4,6},{5,7},{6,0},{7,1},{8,10},{9,11},{10,... | collective-permute-start | bytes 1253384 | tf_op jit(solution)/shard_map/ppermute | solution.py:38
  140.7 33.0 %collective-permute-start.13 = (f32[64,3072]{1,0:T(8,128)S(1)}, f32[64,3072]{1,0:T(8,128)S(1)}, u32[]{:S(2)}, u32[]{:S(2)}) collective-permute-start(f32[64,3072]{1,0:T(8,128)S(1)} %get-tuple-element.23), channel_id=1, source_target_pairs={{0,1},{1,0},{2,3},{3,2},{4,5},{5,4},{6,7},{7,6},{8,9},{9,8},{10,11... | collective-permute-start | bytes 2359304 | tf_op jit(solution)/shard_map/ppermute | solution.py:38
  152.6 21.1 %collective-permute-start.19 = (s16[72,3072]{1,0:T(8,128)(2,1)S(1)}, s16[72,3072]{1,0:T(8,128)(2,1)S(1)}, u32[]{:S(2)}, u32[]{:S(2)}) collective-permute-start(s16[72,3072]{1,0:T(8,128)(2,1)S(1)} %get-tuple-element.29), channel_id=1, source_target_pairs={{0,9},{1,8},{2,11},{3,10},{4,13},{5,12},{6,15},{7,14},{8,1},{9,0},... | collective-permute-start | bytes 1327112 | tf_op jit(solution)/shard_map/ppermute | solution.py:38
  (23 other events, 211.9 us)

commit v3 on v2

--- a/solution.py
+++ b/solution.py
@@ -318,21 +318,23 @@
     tg = 1024
     steps = units // tg // 2
 
-    def grad(base, far, *before):
+    def grad(base, count, far, *before):
         return pl.pallas_call(
             partial(grad_kernel, base), out_shape=S((slab, units), BF16),
             grid_spec=pltpu.PrefetchScalarGridSpec(
-                num_scalar_prefetch=1, grid=(steps,),
-                in_specs=[pl.BlockSpec((64, tg), lambda i, s: (0, i + base))] * 12 + [pl.BlockSpec((64, tg), lambda i, s: (0, i))] * 4
+                num_scalar_prefetch=1, grid=(count,),
+                in_specs=[pl.BlockSpec((64, tg), lambda i, s: (0, i + base))] * 12 + [pl.BlockSpec((64, tg), lambda i, s: (0, i + base % steps))] * 4
                 + [vmem()] + [pl.BlockSpec(memory_space=pl.ANY)] * len(before),
                 out_specs=pl.BlockSpec((slab, tg), lambda i, s: (0, i + base)), scratch_shapes=[V((1024, tg), BF16)],
             ),
             compiler_params=pltpu.CompilerParams(vmem_limit_bytes=24 << 20),
-            cost_estimate=pl.CostEstimate(flops=1024 * slab * units, bytes_accessed=1 << 20, transcendentals=0),
+            cost_estimate=pl.CostEstimate(flops=2 * 1024 * slab * tg * count, bytes_accessed=1 << 20, transcendentals=0),
             input_output_aliases={18: 0} if before else {},
         )(ids, *h_near, *s_near, *far, p_t, *before)
 
-    weight_grad = grad(steps, h_right + s_right, grad(0, h_left + s_left))
+    weight_grad = grad(0, steps, h_left + s_left)
+    weight_grad = grad(steps, steps - 1, h_right + s_right, weight_grad)
+    weight_grad = grad(2 * steps - 1, 1, h_right + s_right, weight_grad)
     return (activation, weight_grad)
 
 

time: 176 us -> 176 us (level)
    pallas_call x2 -> x3, Pallas kernels: 15.6 us -> 17.1 us  [grad(): pl.pallas_call(partial(grad_kernel, base), out_shape=S((slab, units), BF1...]
where the time goes in v3:
time: 176 us
  waiting for transfers between devices  70.2 us (40%)
  starting transfers between devices  52.9 us (30%)
  Pallas kernels  48.7 us (28%)
  other arithmetic  1.93 us (1%)
    ppermute x43, waiting for transfers between devices, send(): return lax.ppermute(a, ('row', 'col'), p)  70.2 us
    ppermute x43, starting transfers between devices, send(): return lax.ppermute(a, ('row', 'col'), p)  52.9 us
    pallas_call x13, Pallas kernels, run(): return g(ids, *args)  31.6 us
    pallas_call x3, Pallas kernels, grad(): pl.pallas_call(partial(grad_kernel, base), out_shape=S((slab, units), BF1...  17.1 us
  transfers between devices with their start and end apart: 43, of which 12 were waited for; matrix products, arithmetic and copies ran while one was open for 1% of the time, Pallas kernels for 26%

profile of v3, /device:TPU:97, one launch (start us, length us, event | category | flops | bytes accessed | tf_op | source)
XLA Modules:
  0.0 176.1 jit_solution(7653185361147424413)
XLA Ops:
  1.4 2.7 %collective-permute-start.21 = (bf16[64,6144]{1,0:T(8,128)(2,1)}, bf16[64,6144]{1,0:T(8,128)(2,1)S(1)}, u32[]{:S(2)}, u32[]{:S(2)}) collective-permute-start(bf16[64,6144]{1,0:T(8,128)(2,1)} %refs_0_.5), channel_id=1, source_target_pairs={{0,6},{1,7},{2,0},{3,1},{4,2},{5,3},{6,4},{7,5},{8,14},{9,15},{10,... | collective-permute-start | bytes 2359304 | tf_op jit(solution)/shard_map/ppermute | solution.py:38
  4.1 2.7 %collective-permute-start = (bf16[128,768]{1,0:T(8,128)(2,1)}, bf16[128,768]{1,0:T(8,128)(2,1)S(1)}, u32[]{:S(2)}, u32[]{:S(2)}) collective-permute-start(bf16[128,768]{1,0:T(8,128)(2,1)} %param.5), channel_id=1, source_target_pairs={{0,64},{1,65},{2,66},{3,67},{4,68},{5,69},{6,70},{7,71},{8,72},{9,... | collective-permute-start | bytes 589832 | tf_op jit(solution)/shard_map/ppermute | solution.py:38
  6.9 5.1 %collective-permute-done = bf16[128,768]{1,0:T(8,128)(2,1)S(1)} collective-permute-done((bf16[128,768]{1,0:T(8,128)(2,1)}, bf16[128,768]{1,0:T(8,128)(2,1)S(1)}, u32[]{:S(2)}, u32[]{:S(2)}) %collective-permute-start) | collective-permute-done | bytes 196640 | tf_op jit(solution)/shard_map/ppermute | solution.py:38
  13.2 2.7 %collective-permute-start.35 = (bf16[128,768]{1,0:T(8,128)(2,1)}, bf16[128,768]{1,0:T(8,128)(2,1)S(1)}, u32[]{:S(2)}, u32[]{:S(2)}) collective-permute-start(bf16[128,768]{1,0:T(8,128)(2,1)} %param.6), channel_id=1, source_target_pairs={{0,64},{1,65},{2,66},{3,67},{4,68},{5,69},{6,70},{7,71},{8,72},{9,... | collective-permute-start | bytes 589832 | tf_op jit(solution)/shard_map/ppermute | solution.py:38
  24.1 3.4 %collective-permute-start.8 = (bf16[2,128,768]{2,1,0:T(8,128)(2,1)S(1)}, bf16[2,128,768]{2,1,0:T(8,128)(2,1)S(1)}, u32[]{:S(2)}, u32[]{:S(2)}) collective-permute-start(bf16[2,128,768]{2,1,0:T(8,128)(2,1)S(1)} %collective-permute-done.7.refs_0_), channel_id=1, source_target_pairs={{0,1},{1,0},{2,3},{3,2},{4,5},{5,4},{6,7},{7,6},{8,9},{9,8},{10,11... | collective-permute-start | bytes 1179656 | tf_op jit(solution)/shard_map/ppermute | solution.py:38
  28.7 3.1 %shard_map.68.refs_2_.refs_4_ = bf16[768,3072]{1,0:T(8,128)(2,1)S(1)} custom-call(s32[8]{0:T(128)} %stack.46.ids, bf16[768,6144]{1,0:T(8,128)(2,1)} %w.1), custom_call_target="tpu_custom_call" | custom-call | flops 1048576 | bytes 1048576 | tf_op jit(solution)/shard_map/pallas_call | solution.py:254
  32.9 2.9 %shard_map.69.refs_3_.refs_5_ = bf16[768,3072]{1,0:T(8,128)(2,1)S(1)} custom-call(s32[8]{0:T(128)S(1)} %copy-done.1, bf16[768,6144]{1,0:T(8,128)(2,1)} %collective-permute-done.2.w), custom_call_target="tpu_custom_call" | custom-call | flops 1048576 | bytes 1048576 | tf_op jit(solution)/shard_map/pallas_call | solution.py:254
  39.5 3.2 %shard_map.70.refs_0_ = f32[256,3072]{1,0:T(8,128)S(1)} custom-call(s32[8]{0:T(128)S(1)} %copy-done.1, bf16[2,128,768]{2,1,0:T(8,128)(2,1)S(1)} %pad_maximum_fusion.refs_0_, bf16[2,128,768]{2,1,0:T(8,128)(2,1)S(1)} %collective-permute-done.1.refs_1_, bf16[768,3072]{1,0:T(8,128)(2,1)S(1)} %shard_map.68.refs_2_.refs_4_, ...), custom_call_target="tpu_custom_call" | custom-call | flops 2415919104 | bytes 1048576 | tf_op jit(solution)/shard_map/pallas_call | solution.py:254
  42.7 3.2 %shard_map.72.refs_3_ = f32[256,3072]{1,0:T(8,128)S(1)} custom-call(s32[8]{0:T(128)S(1)} %copy-done.1, bf16[2,128,768]{2,1,0:T(8,128)(2,1)S(1)} %collective-permute-done.7.refs_0_, bf16[2,128,768]{2,1,0:T(8,128)(2,1)S(1)} %collective-permute-done.8.refs_1_, bf16[768,3072]{1,0:T(8,128)(2,1)S(1)} %shard_map.68.refs_2_.refs_4_, ...), custom_call_target="tpu_custom_call" | custom-call | flops 2415919104 | bytes 1048576 | tf_op jit(solution)/shard_map/pallas_call | solution.py:254
  48.7 3.9 %collective-permute-start.38 = (bf16[2,128,768]{2,1,0:T(8,128)(2,1)S(1)}, bf16[2,128,768]{2,1,0:T(8,128)(2,1)S(1)}, u32[]{:S(2)}, u32[]{:S(2)}) collective-permute-start(bf16[2,128,768]{2,1,0:T(8,128)(2,1)S(1)} %pad_maximum_fusion.1.p0), channel_id=1, source_target_pairs={{0,32},{1,33},{2,34},{3,35},{4,36},{5,37},{6,38},{7,39},{8,40},{9,... | collective-permute-start | bytes 1179656 | tf_op jit(solution)/shard_map/ppermute | solution.py:38
  52.9 6.7 %shard_map.71 = (f32[256,3072]{1,0:T(8,128)S(1)}, f32[256,3072]{1,0:T(8,128)S(1)}) custom-call(s32[8]{0:T(128)S(1)} %copy-done.1, bf16[2,128,768]{2,1,0:T(8,128)(2,1)} %collective-permute-done.3.refs_0_, bf16[2,128,768]{2,1,0:T(8,128)(2,1)} %collective-permute-done.4.refs_1_, bf16[2,128,768]{2,1,0:T(8,128)(2,1)S(1)} %collective-permute-done.5.refs_2_, ...), custom_call_target="tpu_custom_call" | custom-call | flops 4831838208 | bytes 1048576 | tf_op jit(solution)/shard_map/pallas_call | solution.py:254
  60.6 2.8 %collective-permute-start.31 = (bf16[64,3072]{1,0:T(8,128)(2,1)S(1)}, bf16[64,3072]{1,0:T(8,128)(2,1)S(1)}, u32[]{:S(2)}, u32[]{:S(2)}) collective-permute-start(bf16[64,3072]{1,0:T(8,128)(2,1)S(1)} %slice.8), channel_id=1, source_target_pairs={{0,6},{1,7},{2,0},{3,1},{4,2},{5,3},{6,4},{7,5},{8,14},{9,15},{10,... | collective-permute-start | bytes 1179656 | tf_op jit(solution)/shard_map/ppermute | solution.py:38
  65.1 5.2 %collective-permute-done.38.p3 = bf16[2,128,768]{2,1,0:T(8,128)(2,1)S(1)} collective-permute-done((bf16[2,128,768]{2,1,0:T(8,128)(2,1)S(1)}, bf16[2,128,768]{2,1,0:T(8,128)(2,1)S(1)}, u32[]{:S(2)}, u32[]{:S(2)}) %collective-permute-start.38) | collective-permute-done | bytes 393248 | tf_op jit(solution)/shard_map/ppermute | solution.py:38
  73.4 25.3 %collective-permute-done.39.refs_12_ = bf16[64,3072]{1,0:T(8,128)(2,1)S(1)} collective-permute-done((bf16[64,3072]{1,0:T(8,128)(2,1)S(1)}, bf16[64,3072]{1,0:T(8,128)(2,1)S(1)}, u32[]{:S(2)}, u32[]{:S(2)}) %collective-permute-start.39) | collective-permute-done | bytes 393248 | tf_op jit(solution)/shard_map/ppermute | solution.py:38
  104.0 2.7 %collective-permute-start.12 = (s16[136,3072]{1,0:T(8,128)(2,1)S(1)}, s16[136,3072]{1,0:T(8,128)(2,1)S(1)}, u32[]{:S(2)}, u32[]{:S(2)}) collective-permute-start(s16[136,3072]{1,0:T(8,128)(2,1)S(1)} %get-tuple-element.21), channel_id=1, source_target_pairs={{0,6},{1,7},{2,0},{3,1},{4,2},{5,3},{6,4},{7,5},{8,14},{9,15},{10,... | collective-permute-start | bytes 2506760 | tf_op jit(solution)/shard_map/ppermute | solution.py:38
  109.4 7.3 %collective-permute-done.32.refs_13_ = bf16[64,3072]{1,0:T(8,128)(2,1)S(1)} collective-permute-done((bf16[64,3072]{1,0:T(8,128)(2,1)S(1)}, bf16[64,3072]{1,0:T(8,128)(2,1)S(1)}, u32[]{:S(2)}, u32[]{:S(2)}) %collective-permute-start.32) | collective-permute-done | bytes 393248 | tf_op jit(solution)/shard_map/ppermute | solution.py:38
  119.4 5.8 %collective-permute-done.40.refs_13_ = bf16[64,3072]{1,0:T(8,128)(2,1)S(1)} collective-permute-done((bf16[64,3072]{1,0:T(8,128)(2,1)S(1)}, bf16[64,3072]{1,0:T(8,128)(2,1)S(1)}, u32[]{:S(2)}, u32[]{:S(2)}) %collective-permute-start.40) | collective-permute-done | bytes 393248 | tf_op jit(solution)/shard_map/ppermute | solution.py:38
  128.3 2.7 %collective-permute-start.15 = (s16[136,1536]{1,0:T(8,128)(2,1)S(1)}, s16[136,1536]{1,0:T(8,128)(2,1)S(1)}, u32[]{:S(2)}, u32[]{:S(2)}) collective-permute-start(s16[136,1536]{1,0:T(8,128)(2,1)S(1)} %get-tuple-element.25), channel_id=1, source_target_pairs={{0,6},{1,7},{2,0},{3,1},{4,2},{5,3},{6,4},{7,5},{8,14},{9,15},{10,... | collective-permute-start | bytes 1253384 | tf_op jit(solution)/shard_map/ppermute | solution.py:38
  134.7 6.0 %collective-permute-done.14.refs_4_ = s16[136,1536]{1,0:T(8,128)(2,1)S(1)} collective-permute-done((s16[136,1536]{1,0:T(8,128)(2,1)S(1)}, s16[136,1536]{1,0:T(8,128)(2,1)S(1)}, u32[]{:S(2)}, u32[]{:S(2)}) %collective-permute-start.14) | collective-permute-done | bytes 417824 | tf_op jit(solution)/shard_map/ppermute | solution.py:38
  142.0 7.8 %shard_map.81.refs_17_ = bf16[768,6144]{1,0:T(8,128)(2,1)} custom-call(s32[8]{0:T(128)S(1)} %copy-done.1, bf16[64,6144]{1,0:T(8,128)(2,1)S(1)} %copy-done, bf16[64,6144]{1,0:T(8,128)(2,1)S(1)} %collective-permute-done.20.refs_1_, bf16[64,6144]{1,0:T(8,128)(2,1)S(1)} %collective-permute-done.21.refs_2_, bf16[64,6144]{1,0:T(8,128)(2,1)S(1)} %collective-permute-done.22.refs_3_, ...), custom_call_target="tpu_custom_call" | custom-call | flops 4831838208 | bytes 1048576 | tf_op jit(solution)/shard_map/pallas_call | solution.py:322
  152.6 3.6 %collective-permute-start.19 = (s16[72,3072]{1,0:T(8,128)(2,1)S(1)}, s16[72,3072]{1,0:T(8,128)(2,1)S(1)}, u32[]{:S(2)}, u32[]{:S(2)}) collective-permute-start(s16[72,3072]{1,0:T(8,128)(2,1)S(1)} %get-tuple-element.29), channel_id=1, source_target_pairs={{0,9},{1,8},{2,11},{3,10},{4,13},{5,12},{6,15},{7,14},{8,1},{9,0},... | collective-permute-start | bytes 1327112 | tf_op jit(solution)/shard_map/ppermute | solution.py:38
  156.2 5.8 %shard_map.82.refs_17_ = bf16[768,6144]{1,0:T(8,128)(2,1)} custom-call(s32[8]{0:T(128)S(1)} %copy-done.1, bf16[64,6144]{1,0:T(8,128)(2,1)S(1)} %copy-done, bf16[64,6144]{1,0:T(8,128)(2,1)S(1)} %collective-permute-done.20.refs_1_, bf16[64,6144]{1,0:T(8,128)(2,1)S(1)} %collective-permute-done.21.refs_2_, ...), custom_call_target="tpu_custom_call", output_to_operand_aliasing={{}: (18, {})} | custom-call | flops 3221225472 | bytes 1048576 | tf_op jit(solution)/shard_map/pallas_call | solution.py:322
  161.9 3.5 %shard_map.83 = bf16[768,6144]{1,0:T(8,128)(2,1)} custom-call(s32[8]{0:T(128)S(1)} %copy-done.1, bf16[64,6144]{1,0:T(8,128)(2,1)S(1)} %copy-done, bf16[64,6144]{1,0:T(8,128)(2,1)S(1)} %collective-permute-done.20.refs_1_, bf16[64,6144]{1,0:T(8,128)(2,1)S(1)} %collective-permute-done.21.refs_2_, ...), custom_call_target="tpu_custom_call", output_to_operand_aliasing={{}: (18, {})} | custom-call | flops 1610612736 | bytes 1048576 | tf_op jit(solution)/shard_map/pallas_call | solution.py:322
  165.4 8.3 %collective-permute-done.19.x_sib = s16[72,3072]{1,0:T(8,128)(2,1)S(1)} collective-permute-done((s16[72,3072]{1,0:T(8,128)(2,1)S(1)}, s16[72,3072]{1,0:T(8,128)(2,1)S(1)}, u32[]{:S(2)}, u32[]{:S(2)}) %collective-permute-start.19) | collective-permute-done | bytes 442400 | tf_op jit(solution)/shard_map/ppermute | solution.py:38
  (91 shorter events, 48.0 us)
Async XLA Ops:
  0.6 26.8 %collective-permute-start.2 = (bf16[768,6144]{1,0:T(8,128)(2,1)}, bf16[768,6144]{1,0:T(8,128)(2,1)}, u32[]{:S(2)}, u32[]{:S(2)}) collective-permute-start(bf16[768,6144]{1,0:T(8,128)(2,1)} %w.1), channel_id=1, source_target_pairs={{0,1},{1,0},{2,3},{3,2},{4,5},{5,4},{6,7},{7,6},{8,9},{9,8},{10,11... | collective-permute-start | bytes 28311560 | tf_op jit(solution)/shard_map/ppermute | solution.py:38
  1.4 22.7 %collective-permute-start.21 = (bf16[64,6144]{1,0:T(8,128)(2,1)}, bf16[64,6144]{1,0:T(8,128)(2,1)S(1)}, u32[]{:S(2)}, u32[]{:S(2)}) collective-permute-start(bf16[64,6144]{1,0:T(8,128)(2,1)} %refs_0_.5), channel_id=1, source_target_pairs={{0,6},{1,7},{2,0},{3,1},{4,2},{5,3},{6,4},{7,5},{8,14},{9,15},{10,... | collective-permute-start | bytes 2359304 | tf_op jit(solution)/shard_map/ppermute | solution.py:38
  16.0 19.8 %collective-permute-start.1 = (bf16[2,128,768]{2,1,0:T(8,128)(2,1)S(1)}, bf16[2,128,768]{2,1,0:T(8,128)(2,1)S(1)}, u32[]{:S(2)}, u32[]{:S(2)}) collective-permute-start(bf16[2,128,768]{2,1,0:T(8,128)(2,1)S(1)} %pad_maximum_fusion.refs_0_), channel_id=1, source_target_pairs={{0,1},{1,0},{2,3},{3,2},{4,5},{5,4},{6,7},{7,6},{8,9},{9,8},{10,11... | collective-permute-start | bytes 1179656 | tf_op jit(solution)/shard_map/ppermute | solution.py:38
  19.9 17.2 %collective-permute-start.3 = (bf16[2,128,768]{2,1,0:T(8,128)(2,1)S(1)}, bf16[2,128,768]{2,1,0:T(8,128)(2,1)}, u32[]{:S(2)}, u32[]{:S(2)}) collective-permute-start(bf16[2,128,768]{2,1,0:T(8,128)(2,1)S(1)} %pad_maximum_fusion.refs_0_), channel_id=1, source_target_pairs={{0,16},{1,17},{2,18},{3,19},{4,20},{5,21},{6,22},{7,23},{8,24},{9,... | collective-permute-start | bytes 1179656 | tf_op jit(solution)/shard_map/ppermute | solution.py:38
  24.1 15.3 %collective-permute-start.8 = (bf16[2,128,768]{2,1,0:T(8,128)(2,1)S(1)}, bf16[2,128,768]{2,1,0:T(8,128)(2,1)S(1)}, u32[]{:S(2)}, u32[]{:S(2)}) collective-permute-start(bf16[2,128,768]{2,1,0:T(8,128)(2,1)S(1)} %collective-permute-done.7.refs_0_), channel_id=1, source_target_pairs={{0,1},{1,0},{2,3},{3,2},{4,5},{5,4},{6,7},{7,6},{8,9},{9,8},{10,11... | collective-permute-start | bytes 1179656 | tf_op jit(solution)/shard_map/ppermute | solution.py:38
  27.4 21.3 %collective-permute-start.20 = (bf16[64,6144]{1,0:T(8,128)(2,1)}, bf16[64,6144]{1,0:T(8,128)(2,1)S(1)}, u32[]{:S(2)}, u32[]{:S(2)}) collective-permute-start(bf16[64,6144]{1,0:T(8,128)(2,1)} %refs_0_.5), channel_id=1, source_target_pairs={{0,2},{1,3},{2,4},{3,5},{4,6},{5,7},{6,0},{7,1},{8,10},{9,11},{10,... | collective-permute-start | bytes 2359304 | tf_op jit(solution)/shard_map/ppermute | solution.py:38
  35.9 34.5 %collective-permute-start.22 = (bf16[64,6144]{1,0:T(8,128)(2,1)S(1)}, bf16[64,6144]{1,0:T(8,128)(2,1)S(1)}, u32[]{:S(2)}, u32[]{:S(2)}) collective-permute-start(bf16[64,6144]{1,0:T(8,128)(2,1)S(1)} %copy-done), channel_id=1, source_target_pairs={{0,8},{1,9},{2,10},{3,11},{4,12},{5,13},{6,14},{7,15},{8,0},{9,1},... | collective-permute-start | bytes 2359304 | tf_op jit(solution)/shard_map/ppermute | solution.py:38
  47.4 24.3 %collective-permute-start.25 = (bf16[64,6144]{1,0:T(8,128)(2,1)S(1)}, bf16[64,6144]{1,0:T(8,128)(2,1)S(1)}, u32[]{:S(2)}, u32[]{:S(2)}) collective-permute-start(bf16[64,6144]{1,0:T(8,128)(2,1)S(1)} %copy-done), channel_id=1, source_target_pairs={{0,1},{1,0},{2,3},{3,2},{4,5},{5,4},{6,7},{7,6},{8,9},{9,8},{10,11... | collective-permute-start | bytes 2359304 | tf_op jit(solution)/shard_map/ppermute | solution.py:38
  48.7 21.6 %collective-permute-start.38 = (bf16[2,128,768]{2,1,0:T(8,128)(2,1)S(1)}, bf16[2,128,768]{2,1,0:T(8,128)(2,1)S(1)}, u32[]{:S(2)}, u32[]{:S(2)}) collective-permute-start(bf16[2,128,768]{2,1,0:T(8,128)(2,1)S(1)} %pad_maximum_fusion.1.p0), channel_id=1, source_target_pairs={{0,32},{1,33},{2,34},{3,35},{4,36},{5,37},{6,38},{7,39},{8,40},{9,... | collective-permute-start | bytes 1179656 | tf_op jit(solution)/shard_map/ppermute | solution.py:38
  52.6 47.7 %collective-permute-start.23 = (bf16[64,6144]{1,0:T(8,128)(2,1)S(1)}, bf16[64,6144]{1,0:T(8,128)(2,1)S(1)}, u32[]{:S(2)}, u32[]{:S(2)}) collective-permute-start(bf16[64,6144]{1,0:T(8,128)(2,1)S(1)} %collective-permute-done.20.refs_1_), channel_id=1, source_target_pairs={{0,8},{1,9},{2,10},{3,11},{4,12},{5,13},{6,14},{7,15},{8,0},{9,1},... | collective-permute-start | bytes 2359304 | tf_op jit(solution)/shard_map/ppermute | solution.py:38
  70.2 30.1 %collective-permute-start.9 = (s16[264,1536]{1,0:T(8,128)(2,1)S(1)}, s16[264,1536]{1,0:T(8,128)(2,1)S(1)}, u32[]{:S(2)}, u32[]{:S(2)}) collective-permute-start(s16[264,1536]{1,0:T(8,128)(2,1)S(1)} %get-tuple-element.18), channel_id=1, source_target_pairs={{0,2},{1,3},{2,4},{3,5},{4,6},{5,7},{6,0},{7,1},{8,10},{9,11},{10,... | collective-permute-start | bytes 2433032 | tf_op jit(solution)/shard_map/ppermute | solution.py:38
  70.3 28.3 %collective-permute-start.39 = (bf16[64,3072]{1,0:T(8,128)(2,1)S(1)}, bf16[64,3072]{1,0:T(8,128)(2,1)S(1)}, u32[]{:S(2)}, u32[]{:S(2)}) collective-permute-start(bf16[64,3072]{1,0:T(8,128)(2,1)S(1)} %slice.9), channel_id=1, source_target_pairs={{0,2},{1,3},{2,4},{3,5},{4,6},{5,7},{6,0},{7,1},{8,10},{9,11},{10,... | collective-permute-start | bytes 1179656 | tf_op jit(solution)/shard_map/ppermute | solution.py:38
  71.7 30.7 %collective-permute-start.11 = (s16[264,1536]{1,0:T(8,128)(2,1)S(1)}, s16[264,1536]{1,0:T(8,128)(2,1)S(1)}, u32[]{:S(2)}, u32[]{:S(2)}) collective-permute-start(s16[264,1536]{1,0:T(8,128)(2,1)S(1)} %get-tuple-element.20), channel_id=1, source_target_pairs={{0,6},{1,7},{2,0},{3,1},{4,2},{5,3},{6,4},{7,5},{8,14},{9,15},{10,... | collective-permute-start | bytes 2433032 | tf_op jit(solution)/shard_map/ppermute | solution.py:38
  73.1 30.9 %collective-permute-start.24 = (bf16[64,6144]{1,0:T(8,128)(2,1)S(1)}, bf16[64,6144]{1,0:T(8,128)(2,1)S(1)}, u32[]{:S(2)}, u32[]{:S(2)}) collective-permute-start(bf16[64,6144]{1,0:T(8,128)(2,1)S(1)} %collective-permute-done.21.refs_2_), channel_id=1, source_target_pairs={{0,8},{1,9},{2,10},{3,11},{4,12},{5,13},{6,14},{7,15},{8,0},{9,1},... | collective-permute-start | bytes 2359304 | tf_op jit(solution)/shard_map/ppermute | solution.py:38
  102.4 25.9 %collective-permute-start.10 = (s16[136,3072]{1,0:T(8,128)(2,1)S(1)}, s16[136,3072]{1,0:T(8,128)(2,1)S(1)}, u32[]{:S(2)}, u32[]{:S(2)}) collective-permute-start(s16[136,3072]{1,0:T(8,128)(2,1)S(1)} %get-tuple-element.19), channel_id=1, source_target_pairs={{0,2},{1,3},{2,4},{3,5},{4,6},{5,7},{6,0},{7,1},{8,10},{9,11},{10,... | collective-permute-start | bytes 2506760 | tf_op jit(solution)/shard_map/ppermute | solution.py:38
  104.0 27.0 %collective-permute-start.12 = (s16[136,3072]{1,0:T(8,128)(2,1)S(1)}, s16[136,3072]{1,0:T(8,128)(2,1)S(1)}, u32[]{:S(2)}, u32[]{:S(2)}) collective-permute-start(s16[136,3072]{1,0:T(8,128)(2,1)S(1)} %get-tuple-element.21), channel_id=1, source_target_pairs={{0,6},{1,7},{2,0},{3,1},{4,2},{5,3},{6,4},{7,5},{8,14},{9,15},{10,... | collective-permute-start | bytes 2506760 | tf_op jit(solution)/shard_map/ppermute | solution.py:38
  107.0 18.2 %collective-permute-start.40 = (bf16[64,3072]{1,0:T(8,128)(2,1)S(1)}, bf16[64,3072]{1,0:T(8,128)(2,1)S(1)}, u32[]{:S(2)}, u32[]{:S(2)}) collective-permute-start(bf16[64,3072]{1,0:T(8,128)(2,1)S(1)} %collective-permute-done.39.refs_12_), channel_id=1, source_target_pairs={{0,8},{1,9},{2,10},{3,11},{4,12},{5,13},{6,14},{7,15},{8,0},{9,1},... | collective-permute-start | bytes 1179656 | tf_op jit(solution)/shard_map/ppermute | solution.py:38
  108.2 20.0 %collective-permute-start.41 = (bf16[64,3072]{1,0:T(8,128)(2,1)S(1)}, bf16[64,3072]{1,0:T(8,128)(2,1)S(1)}, u32[]{:S(2)}, u32[]{:S(2)}) collective-permute-start(bf16[64,3072]{1,0:T(8,128)(2,1)S(1)} %collective-permute-done.39.refs_12_), channel_id=1, source_target_pairs={{0,1},{1,0},{2,3},{3,2},{4,5},{5,4},{6,7},{7,6},{8,9},{9,8},{10,11... | collective-permute-start | bytes 1179656 | tf_op jit(solution)/shard_map/ppermute | solution.py:38
  116.8 17.4 %collective-permute-start.29 = (bf16[64,6144]{1,0:T(8,128)(2,1)S(1)}, bf16[64,6144]{1,0:T(8,128)(2,1)S(1)}, u32[]{:S(2)}, u32[]{:S(2)}) collective-permute-start(bf16[64,6144]{1,0:T(8,128)(2,1)S(1)} %collective-permute-done.23.refs_4_), channel_id=1, source_target_pairs={{0,1},{1,0},{2,3},{3,2},{4,5},{5,4},{6,7},{7,6},{8,9},{9,8},{10,11... | collective-permute-start | bytes 2359304 | tf_op jit(solution)/shard_map/ppermute | solution.py:38
  133.9 22.3 %collective-permute-start.33 = (bf16[64,3072]{1,0:T(8,128)(2,1)S(1)}, bf16[64,3072]{1,0:T(8,128)(2,1)S(1)}, u32[]{:S(2)}, u32[]{:S(2)}) collective-permute-start(bf16[64,3072]{1,0:T(8,128)(2,1)S(1)} %collective-permute-done.31.refs_12_), channel_id=1, source_target_pairs={{0,1},{1,0},{2,3},{3,2},{4,5},{5,4},{6,7},{7,6},{8,9},{9,8},{10,11... | collective-permute-start | bytes 1179656 | tf_op jit(solution)/shard_map/ppermute | solution.py:38
  134.2 22.0 %collective-permute-start.34 = (bf16[64,3072]{1,0:T(8,128)(2,1)S(1)}, bf16[64,3072]{1,0:T(8,128)(2,1)S(1)}, u32[]{:S(2)}, u32[]{:S(2)}) collective-permute-start(bf16[64,3072]{1,0:T(8,128)(2,1)S(1)} %collective-permute-done.32.refs_13_), channel_id=1, source_target_pairs={{0,1},{1,0},{2,3},{3,2},{4,5},{5,4},{6,7},{7,6},{8,9},{9,8},{10,11... | collective-permute-start | bytes 1179656 | tf_op jit(solution)/shard_map/ppermute | solution.py:38
  134.7 15.2 %collective-permute-start.16 = (s16[136,1536]{1,0:T(8,128)(2,1)S(1)}, s16[136,1536]{1,0:T(8,128)(2,1)S(1)}, u32[]{:S(2)}, u32[]{:S(2)}) collective-permute-start(s16[136,1536]{1,0:T(8,128)(2,1)S(1)} %get-tuple-element.26), channel_id=1, source_target_pairs={{0,2},{1,3},{2,4},{3,5},{4,6},{5,7},{6,0},{7,1},{8,10},{9,11},{10,... | collective-permute-start | bytes 1253384 | tf_op jit(solution)/shard_map/ppermute | solution.py:38
  140.7 33.0 %collective-permute-start.13 = (f32[64,3072]{1,0:T(8,128)S(1)}, f32[64,3072]{1,0:T(8,128)S(1)}, u32[]{:S(2)}, u32[]{:S(2)}) collective-permute-start(f32[64,3072]{1,0:T(8,128)S(1)} %get-tuple-element.23), channel_id=1, source_target_pairs={{0,1},{1,0},{2,3},{3,2},{4,5},{5,4},{6,7},{7,6},{8,9},{9,8},{10,11... | collective-permute-start | bytes 2359304 | tf_op jit(solution)/shard_map/ppermute | solution.py:38
  152.6 21.1 %collective-permute-start.19 = (s16[72,3072]{1,0:T(8,128)(2,1)S(1)}, s16[72,3072]{1,0:T(8,128)(2,1)S(1)}, u32[]{:S(2)}, u32[]{:S(2)}) collective-permute-start(s16[72,3072]{1,0:T(8,128)(2,1)S(1)} %get-tuple-element.29), channel_id=1, source_target_pairs={{0,9},{1,8},{2,11},{3,10},{4,13},{5,12},{6,15},{7,14},{8,1},{9,0},... | collective-permute-start | bytes 1327112 | tf_op jit(solution)/shard_map/ppermute | solution.py:38
  (23 other events, 213.4 us)
